TPU v7x, 512 devices: a whole 4x8x8 slice. The times are simulated.
512 devices in a mesh: zero: 32 (over y, x), width: 16 (over z, core).
Axes of the slice: x: 4, y: 8, z: 8, core: 2. Of those that a mesh axis runs over, the one named last changes fastest.
Arguments:
- w_gate: bfloat16 [3072, 8192], P('zero', 'width'), may hold values from -0.109375 to 0.109375
- low_gate: bfloat16 [3072, 16], P('zero'), may hold values from -0.109375 to 0.109375
- high_gate: bfloat16 [16, 8192], P(None, 'width'), may hold values from -1.5 to 1.5
- w_up: bfloat16 [3072, 8192], P('zero', 'width'), may hold values from -0.109375 to 0.109375
- low_up: bfloat16 [3072, 16], P('zero'), may hold values from -0.109375 to 0.109375
- high_up: bfloat16 [16, 8192], P(None, 'width'), may hold values from -1.5 to 1.5
- norm_train: float32 [3072], P(('zero', 'width')), may hold values from 0.25 to 1.75
- norm_step: float32 [3072], P(('zero', 'width')), may hold values from -0.3 to 0.3
Outputs:
- serving_gate: bfloat16 [8192, 3072], P('width')
- serving_up: bfloat16 [8192, 3072], P('width')
- serve_norm: bfloat16 [3072], replicated
All inputs are finite; a program needn't handle non-finite values.
Results may differ from a plain program's by a relative error of at most 0.001.
Values may be sent and summed in bfloat16 or wider, within the bound.
No kernel may reach another device: no remote copies, remote signals or barrier semaphores. Data moves between devices by JAX's collectives and lax.ppermute only.
A program may use at most 64 MiB of HBM per device.

v0:
```python
import jax
import jax.numpy as jnp
from jax import lax
from jax.sharding import PartitionSpec as P

mix_rate = 1.0


def in_one_piece(arrays, axis, dim, along):
    ends, at = ([], 0)
    for a in arrays[:-1]:
        at += a.shape[along]
        ends.append(at)
    both = jnp.concatenate(arrays, axis=along)
    return tuple(jnp.split(lax.all_gather(both, axis, axis=dim, tiled=True), ends, axis=along))


def on_device(w_gate, low_gate, high_gate, w_up, low_up, high_up, norm_train, norm_step):
    whole_gate = w_gate.astype(jnp.float32) + mix_rate * jnp.dot(
        low_gate, high_gate, preferred_element_type=jnp.float32
    )
    whole_up = w_up.astype(jnp.float32) + mix_rate * jnp.dot(
        low_up, high_up, preferred_element_type=jnp.float32
    )
    narrow_gate, narrow_up = (whole_gate.astype(jnp.bfloat16), whole_up.astype(jnp.bfloat16))
    serving_gate, serving_up = in_one_piece((narrow_gate, narrow_up), "zero", 0, 1)
    serving_gate, serving_up = (serving_gate.T, serving_up.T)
    serve_norm = lax.all_gather(
        (norm_train + norm_step).astype(jnp.bfloat16), ("zero", "width"), axis=0, tiled=True
    )
    return (serving_gate, serving_up, serve_norm)


def solution(mesh):
    placed = (
        P("zero", "width"),
        P("zero", None),
        P(None, "width"),
        P("zero", "width"),
        P("zero", None),
        P(None, "width"),
        P(("zero", "width")),
        P(("zero", "width")),
    )
    return jax.shard_map(
        on_device,
        mesh=mesh,
        in_specs=placed,
        out_specs=(P("width", None), P("width", None), P()),
        check_vma=False,
    )
```

profile of v0, /device:TPU:1, one launch (start us, length us, event | category | flops | bytes accessed | tf_op | source)
XLA Modules:
  0.0 139.9 jit_solution(1368829376719090924)
XLA Ops:
  7.2 0.0 copy-start
  7.2 0.0 all-gather.2.cloned.1.call-start
  7.2 0.7 copy-done
  7.9 1.1 fusion
  9.0 1.1 fusion.1
  10.1 0.7 pad_maximum_fusion
  10.8 0.0 all-gather.2.cloned.1.call-update
  10.9 0.7 add_convert_fusion
  11.5 0.2 dynamic-update-slice
  11.8 108.7 %all-reduce = bf16[3072]{0:T(1024)(128)(2,1)} all-reduce(bf16[3072]{0:T(1024)(128)(2,1)S(1)} %dynamic-update-slice), channel_id=1, replica_groups=mesh['zero'=32,'width'=16] {'zero','width'}, use_global_device_ids=true, to_apply=%add | all-reduce | flops 3072 | bytes 12288
  120.5 0.0 all-gather.2.cloned.1.call-done
  120.5 4.9 %slice_bitcast_fusion = (bf16[512,3072]{0,1:T(8,128)(2,1)S(1)}, bf16[512,3072]{0,1:T(8,128)(2,1)}) fusion(bf16[3072,1024]{1,0:T(8,128)(2,1)} %all-gather.2.cloned.1.call-done), kind=kLoop, calls=%fused_computation | loop fusion | bytes 12582912 | tf_op jit(solution)/shard_map/transpose | solution.py:27
  125.4 4.6 %copy.11 = bf16[512,3072]{1,0:T(8,128)(2,1)} copy(bf16[512,3072]{0,1:T(8,128)(2,1)} %get-tuple-element.7) | data formatting | bytes 6291456
  130.0 3.0 %copy.12 = bf16[512,3072]{1,0:T(8,128)(2,1)} copy(bf16[512,3072]{0,1:T(8,128)(2,1)S(1)} %get-tuple-element.6) | data formatting | bytes 6291456
  (1 shorter events, 0.0 us)
Async XLA Ops:
  7.2 0.7 copy-start
  7.2 113.3 %all-gather.2.cloned.1.call-start = ((), (), s32[]{:S(2)}) async-start(), calls=%async_computation | async-start | bytes 6488064 | tf_op jit(solution)/shard_map/all_gather | solution.py:15
Sparse Core Ops, SparseCore 0:
  11.7 98.2 all-gather.1
where the time goes:
time: 140 us
  blocking collectives  109 us (78%)
  between operations  14.1 us (10%)
  local copies, waits for them, and re-layouts  13.4 us (10%)
  matrix products  2.23 us (2%)
    unnamed x1, blocking collectives  109 us
    unnamed x6, local copies, waits for them, and re-layouts  8.54 us
    transpose x1, local copies, waits for them, and re-layouts, on_device(): serving_gate, serving_up = (serving_gate.T, serving_up.T)  4.91 us
  transfers between devices with their start and end apart: 1, of which 0 were waited for; matrix products, arithmetic and copies ran while one was open for 1% of the time, Pallas kernels for 0%

commit v1 on v0

v1 whole, which is shorter than its diff:
```python
import jax
import jax.numpy as jnp
from jax import lax
from jax.experimental import pallas as pl
from jax.experimental.pallas import tpu as pltpu
from jax.sharding import PartitionSpec as P

mix_rate = 1.0
LANES, PIECE = 128, 96
NY, NX, NW = 8, 4, 16
N_FIRST = 5
N_LAST = 8 - N_FIRST
ROWS_FIRST = N_FIRST * PIECE + 8
ROWS_LAST = N_LAST * PIECE
X_ROWS = [[y * NX + x for x in range(NX)] for y in range(NY)]
Y_ROWS = [[y * NX + x for y in range(NY)] for x in range(NX)]


def swap(a, step):
    pairs = []
    for y in range(NY):
        for x in range(NX):
            d = 1 if (x + step) % 2 == 0 else -1
            pairs.append((y * NX + x, y * NX + (x + d) % NX))
    return lax.ppermute(a, "zero", pairs)


def merge_kernel(wg, lg, hg, wu, lu, hu, nt, ns, first, last):
    def whole(w, low_t, high):
        prod = lax.dot_general(low_t[...], high[...], (((0,), (0,)), ((), ())), preferred_element_type=jnp.float32)
        return (w[...].astype(jnp.float32) + mix_rate * prod).astype(jnp.bfloat16)

    gate, up = whole(wg, lg, hg), whole(wu, lu, hu)
    n = (nt[...] + ns[...]).astype(jnp.bfloat16)
    eye = (lax.broadcasted_iota(jnp.int32, (6, LANES), 0) == lax.broadcasted_iota(jnp.int32, (6, LANES), 1)).astype(jnp.bfloat16)
    rows = jnp.dot(jnp.broadcast_to(n, (8, 6)), eye, preferred_element_type=jnp.float32).astype(jnp.bfloat16)
    for t in range(8):
        c = (t % 4) * LANES
        tile = (gate if t < 4 else up)[:, c:c + LANES]
        if t < N_FIRST:
            for x in range(NX):
                first[x, t * PIECE:(t + 1) * PIECE, :] = tile
        else:
            last[(t - N_FIRST) * PIECE:(t - N_FIRST + 1) * PIECE, :] = tile
    for x in range(NX):
        first[x, N_FIRST * PIECE:, :] = rows


def last_kernel(pos, *refs):
    ins, (up, stage, blk, sem) = refs[:6], refs[6:]
    x, t = pos[0], pos[1]
    for h in range(2):
        own, near, far = ins[3 * h:3 * h + 3]
        s = t if h == 0 else -t
        at = [(x + m * s + 2 * NX) % NX for m in (0, 1, -1, -2)]

        @pl.loop(0, NY // 2)
        def _(g):
            for i in range(N_LAST):
                r = pl.ds(i * PIECE, PIECE)
                for k, part in enumerate((own[g, r, :], near[g, r, :], far[0, g, r, :], far[1, g, r, :])):
                    blk[i, pl.ds(pl.multiple_of(at[k] * PIECE, 32), PIECE), :] = part
            for i in range(N_LAST):
                stage[h * (NY // 2) + g, i * LANES:(i + 1) * LANES, :] = blk[i].T

    copies = [
        pltpu.make_async_copy(
            stage.at[y],
            up.at[pl.ds(512 - N_LAST * LANES, N_LAST * LANES), pl.ds(y * 384, 384)],
            sem.at[y],
        )
        for y in range(NY)
    ]
    for cp in copies:
        cp.start()
    for cp in copies:
        cp.wait()


def first_kernel(got, up_in, gate, up):
    for t in range(N_FIRST):
        block = jnp.concatenate([got[0, x, t * PIECE:(t + 1) * PIECE, :] for x in range(NX)], axis=0)
        out = gate if t < 4 else up
        out[(t % 4) * LANES:(t % 4 + 1) * LANES, :] = block.T


def norm_kernel(got, out):
    total = jnp.zeros((32, LANES), jnp.float32)
    e = lax.broadcasted_iota(jnp.int32, (LANES, LANES), 0)
    c = lax.broadcasted_iota(jnp.int32, (LANES, LANES), 1)
    for j in range(NW):
        pick = ((c == e + 6 * j) & (e < 6)).astype(jnp.bfloat16)
        total += jnp.dot(got[j], pick, preferred_element_type=jnp.float32)
    out[...] = total.astype(jnp.bfloat16)


def on_device(w_gate, low_gate, high_gate, w_up, low_up, high_up, norm_train, norm_step):
    vm = pl.BlockSpec(memory_space=pltpu.VMEM)
    sm = pl.BlockSpec(memory_space=pltpu.SMEM)
    hb = pl.BlockSpec(memory_space=pl.ANY)
    bf16 = jnp.bfloat16
    x = lax.axis_index("zero") & (NX - 1)
    pos = jnp.stack([x, 1 - 2 * (x & 1)]).astype(jnp.int32)
    first, last = pl.pallas_call(
        merge_kernel, in_specs=[vm] * 8, out_specs=[vm, vm],
        out_shape=[jax.ShapeDtypeStruct((NX, ROWS_FIRST, LANES), bf16), jax.ShapeDtypeStruct((ROWS_LAST, LANES), bf16)],
        name="merge",
    )(w_gate, low_gate.T, high_gate, w_up, low_up.T, high_up, norm_train[None, :], norm_step[None, :])

    along_x = lax.all_to_all(first, "zero", 0, 0, tiled=True, axis_index_groups=X_ROWS)
    got_first = lax.all_gather(along_x, "zero", axis=0, axis_index_groups=Y_ROWS)

    norm_x = along_x[:, N_FIRST * PIECE:, :].reshape(NX * 8, LANES)
    own = jnp.concatenate([last, norm_x], axis=0)
    along_y = lax.all_to_all(
        jnp.broadcast_to(own[None], (NY,) + own.shape), "zero", 0, 0, tiled=True, axis_index_groups=Y_ROWS)

    halves = []
    for h in range(2):
        a = along_y[h * 4:(h + 1) * 4, :ROWS_LAST]
        halves.append((a, swap(a, h)))
    norm_rows = along_y[:, ROWS_LAST:].reshape(32, 8, LANES)[:, 0, :]
    both = [jnp.stack(h) for h in halves]
    *both, norm_rows = lax.optimization_barrier((*both, norm_rows))
    parts = []
    for h in range(2):
        parts += [*halves[h], swap(both[h], 1 - h)]

    spread = lax.all_to_all(jnp.broadcast_to(norm_rows[None], (NW, 32, LANES)), "width", 0, 0, tiled=True)
    norm = pl.pallas_call(
        norm_kernel, in_specs=[vm], out_specs=vm, out_shape=jax.ShapeDtypeStruct((32, LANES), bf16), name="norm",
    )(spread)
    serve_norm = norm[:, :PIECE].reshape(3072)

    out = jax.ShapeDtypeStruct((512, 3072), bf16)
    up = pl.pallas_call(
        last_kernel, in_specs=[sm] + [vm] * 6, out_specs=hb, out_shape=out,
        scratch_shapes=[
            pltpu.VMEM((NY, N_LAST * LANES, 384), bf16),
            pltpu.VMEM((N_LAST, 384, LANES), bf16),
            pltpu.SemaphoreType.DMA((NY,)),
        ],
        name="last",
    )(pos, *parts)
    gate, up = pl.pallas_call(
        first_kernel, grid=(NY,),
        in_specs=[pl.BlockSpec((1, NX, ROWS_FIRST, LANES), lambda y: (y, 0, 0, 0)), hb],
        out_specs=[pl.BlockSpec((512, 384), lambda y: (0, y)), pl.BlockSpec(((N_FIRST - 4) * LANES, 384), lambda y: (0, y))],
        out_shape=[out, out], input_output_aliases={1: 1}, name="first",
    )(got_first, up)
    return (gate, up, serve_norm)


def solution(mesh):
    placed = (
        P("zero", "width"), P("zero", None), P(None, "width"),
        P("zero", "width"), P("zero", None), P(None, "width"),
        P(("zero", "width")), P(("zero", "width")),
    )
    return jax.shard_map(
        on_device, mesh=mesh, in_specs=placed,
        out_specs=(P("width", None), P("width", None), P()), check_vma=False,
    )
```

time: 140 us -> 120 us (0.86)
  blocking collectives: 109 us -> 38.8 us
  starting transfers between devices: 0.04 us -> 31.1 us
  Pallas kernels: 0 us -> 15 us
  waiting for transfers between devices: 0.02 us -> 14.2 us
  local copies, waits for them, and re-layouts: 13.4 us -> 4.62 us
  matrix products: 2.23 us -> 0 us
    unnamed x1 -> x0, blocking collectives: 109 us -> none
    all_to_all x0 -> x2, blocking collectives: none -> 38.8 us  [the longest x1 27 us: on_device(): lax.all_to_all(jnp.broadcast_to(own[None], (NY,) + own.shape), 'zero', 0,...]
    all_to_all x0 -> x1, starting transfers between devices: none -> 20.7 us  [on_device(): lax.all_to_all(jnp.broadcast_to(norm_rows[None], (NW, 32, LANES)), 'width...]
    pallas_call x0 -> x4, Pallas kernels: none -> 15 us  [the longest x1 6.95 us: on_device(): pl.pallas_call(first_kernel, grid=(NY,), in_specs=[pl.BlockSpec((1, NX, R...]
    ppermute x0 -> x4, starting transfers between devices: none -> 10.3 us  [swap(): return lax.ppermute(a, 'zero', pairs)]
    all_to_all x0 -> x1, waiting for transfers between devices: none -> 8.35 us  [on_device(): lax.all_to_all(jnp.broadcast_to(norm_rows[None], (NW, 32, LANES)), 'width...]
    unnamed x6 -> x13, local copies, waits for them, and re-layouts: 8.54 us -> 1.62 us
    ppermute x0 -> x4, waiting for transfers between devices: none -> 5.84 us  [swap(): return lax.ppermute(a, 'zero', pairs)]
  transfers between devices with their start and end apart: 1 -> 6, of which waited for: 0 -> 3; matrix products, arithmetic and copies ran while one was open for 1% -> 4% of each run, Pallas kernels for 0% -> 5%
where the time goes in v1:
time: 120 us
  blocking collectives  38.8 us (32%)
  starting transfers between devices  31.1 us (26%)
  Pallas kernels  15 us (12%)
  waiting for transfers between devices  14.2 us (12%)
  between operations  14.2 us (12%)
  local copies, waits for them, and re-layouts  4.62 us (4%)
  other arithmetic  1.65 us (1%)
    all_to_all x1, blocking collectives, on_device(): lax.all_to_all(jnp.broadcast_to(own[None], (NY,) + own.shape), 'zero', 0,...  27 us
    all_to_all x1, starting transfers between devices, on_device(): lax.all_to_all(jnp.broadcast_to(norm_rows[None], (NW, 32, LANES)), 'width...  20.7 us
    all_to_all x1, blocking collectives, on_device(): lax.all_to_all(first, 'zero', 0, 0, tiled=True, axis_index_groups=X_ROWS)  11.7 us
    ppermute x4, starting transfers between devices, swap(): return lax.ppermute(a, 'zero', pairs)  10.3 us
    all_to_all x1, waiting for transfers between devices, on_device(): lax.all_to_all(jnp.broadcast_to(norm_rows[None], (NW, 32, LANES)), 'width...  8.35 us
    pallas_call x1, Pallas kernels, on_device(): pl.pallas_call(first_kernel, grid=(NY,), in_specs=[pl.BlockSpec((1, NX, R...  6.95 us
    ppermute x4, waiting for transfers between devices, swap(): return lax.ppermute(a, 'zero', pairs)  5.84 us
    pallas_call x1, Pallas kernels, on_device(): pl.pallas_call(last_kernel, in_specs=[sm] + [vm] * 6, out_specs=hb, out_s...  4.36 us
  transfers between devices with their start and end apart: 6, of which 3 were waited for; matrix products, arithmetic and copies ran while one was open for 4% of the time, Pallas kernels for 5%

profile of v1, /device:TPU:1, one launch (start us, length us, event | category | flops | bytes accessed | tf_op | source)
XLA Modules:
  0.0 119.5 jit_solution(10137065974253661431)
XLA Ops:
  7.2 0.0 all-gather.3.cloned.1.call-start
  7.2 2.0 %merge.1 = (bf16[4,488,128]{2,1,0:T(8,128)(2,1)}, bf16[288,128]{1,0:T(8,128)(2,1)}) custom-call(bf16[96,512]{1,0:T(8,128)(2,1)} %wg.1, bf16[16,96]{1,0:T(8,128)(2,1)} %bitcast.26, bf16[16,512]{1,0:T(8,128)(2,1)} %hg.1, bf16[96,512]{1,0:T(8,128)(2,1)} %wu.1, bf16[16,96]{1,0:T(8,128)(2,1)} %bitcast.27, bf16[16,512]{1,0:T(8,128)(2,1)} %hu.1, f32[1,6]{1,0:T(1,128)} %bitcast.28, ...), custom_call_target="tpu_custom_call" | custom-call | tf_op jit(solution)/shard_map/merge/pallas_call | solution.py:104
  9.2 11.7 %all_to_all.15 = bf16[4,488,128]{2,1,0:T(8,128)(2,1)} all-to-all(bf16[4,488,128]{2,1,0:T(8,128)(2,1)} %get-tuple-element.10), channel_id=1, replica_groups={{0,16,32,48},{64,80,96,112},{128,144,160,176},{192,208,224,240},{256,27..., dimensions={0} | all-to-all | bytes 999424 | tf_op jit(solution)/shard_map/all_to_all | solution.py:110
  21.0 0.0 all-gather.3.cloned.1.call-update
  21.0 0.7 slice_bitcast_fusion
  21.7 0.9 pad_maximum_fusion.2
  22.6 0.1 broadcast_in_dim.20
  22.7 27.0 %all_to_all.16 = bf16[8,320,128]{2,1,0:T(8,128)(2,1)S(1)} all-to-all(bf16[8,320,128]{2,1,0:T(8,128)(2,1)S(1)} %broadcast_in_dim.20), channel_id=1, replica_groups={{0,64,128,192,256,320,384,448},{16,80,144,208,272,336,400,464},{32,96,1..., dimensions={0} | all-to-all | bytes 1310720 | tf_op jit(solution)/shard_map/all_to_all | solution.py:115
  49.7 0.2 slice_bitcast_fusion.1
  49.9 2.1 %collective-permute-start.1 = (bf16[4,288,128]{2,1,0:T(8,128)(2,1)S(1)}, bf16[4,288,128]{2,1,0:T(8,128)(2,1)S(1)}, u32[]{:S(2)}, u32[]{:S(2)}) collective-permute-start(bf16[4,288,128]{2,1,0:T(8,128)(2,1)S(1)} %get-tuple-element.19.refs_3_), channel_id=1, source_target_pairs={{0,48},{16,32},{32,16},{48,0},{64,112},{80,96},{96,80},{112,64},{1... | collective-permute-start | bytes 884744 | tf_op jit(solution)/shard_map/ppermute | solution.py:25
  52.0 1.9 %collective-permute-start = (bf16[4,288,128]{2,1,0:T(8,128)(2,1)S(1)}, bf16[4,288,128]{2,1,0:T(8,128)(2,1)S(1)}, u32[]{:S(2)}, u32[]{:S(2)}) collective-permute-start(bf16[4,288,128]{2,1,0:T(8,128)(2,1)S(1)} %get-tuple-element.20.refs_0_), channel_id=1, source_target_pairs={{0,16},{16,0},{32,48},{48,32},{64,80},{80,64},{96,112},{112,96},{1... | collective-permute-start | bytes 884744 | tf_op jit(solution)/shard_map/ppermute | solution.py:25
  54.0 5.0 %collective-permute-done.1.refs_4_ = bf16[4,288,128]{2,1,0:T(8,128)(2,1)S(1)} collective-permute-done((bf16[4,288,128]{2,1,0:T(8,128)(2,1)S(1)}, bf16[4,288,128]{2,1,0:T(8,128)(2,1)S(1)}, u32[]{:S(2)}, u32[]{:S(2)}) %collective-permute-start.1) | collective-permute-done | bytes 294944 | tf_op jit(solution)/shard_map/ppermute | solution.py:25
  59.0 0.1 pad_maximum_fusion.1
  59.0 0.8 collective-permute-done.refs_1_
  59.8 0.1 pad_maximum_fusion
  59.9 4.4 %collective-permute-start.2 = (bf16[2,4,288,128]{3,2,1,0:T(8,128)(2,1)S(1)}, bf16[2,4,288,128]{3,2,1,0:T(8,128)(2,1)S(1)}, u32[]{:S(2)}, u32[]{:S(2)}) collective-permute-start(bf16[2,4,288,128]{3,2,1,0:T(8,128)(2,1)S(1)} %pad_maximum_fusion), channel_id=1, source_target_pairs={{0,48},{16,32},{32,16},{48,0},{64,112},{80,96},{96,80},{112,64},{1... | collective-permute-start | bytes 1769480 | tf_op jit(solution)/shard_map/ppermute | solution.py:25
  64.3 1.9 %collective-permute-start.3 = (bf16[2,4,288,128]{3,2,1,0:T(8,128)(2,1)S(1)}, bf16[2,4,288,128]{3,2,1,0:T(8,128)(2,1)S(1)}, u32[]{:S(2)}, u32[]{:S(2)}) collective-permute-start(bf16[2,4,288,128]{3,2,1,0:T(8,128)(2,1)S(1)} %pad_maximum_fusion.1), channel_id=1, source_target_pairs={{0,16},{16,0},{32,48},{48,32},{64,80},{80,64},{96,112},{112,96},{1... | collective-permute-start | bytes 1769480 | tf_op jit(solution)/shard_map/ppermute | solution.py:25
  66.3 0.7 broadcast_in_dim.21
  66.9 20.7 %all-to-all-start.2 = ((bf16[16,32,128]{2,1,0:T(8,128)(2,1)}), bf16[16,32,128]{2,1,0:T(8,128)(2,1)}, u32[]{:S(2)}, u32[]{:S(2)}) async-start(bf16[16,32,128]{2,1,0:T(8,128)(2,1)} %broadcast_in_dim.21), calls=%async_computation.2 | async-start | bytes 262144 | tf_op jit(solution)/shard_map/all_to_all | solution.py:129
  87.6 0.6 pad_add_fusion.pos
  88.3 8.3 %all-to-all-done.2.got = bf16[16,32,128]{2,1,0:T(8,128)(2,1)} async-done(((bf16[16,32,128]{2,1,0:T(8,128)(2,1)}), bf16[16,32,128]{2,1,0:T(8,128)(2,1)}, u32[]{:S(2)}, u32[]{:S(2)}) %all-to-all-start.2) | async-done | bytes 131104 | tf_op jit(solution)/shard_map/all_to_all | solution.py:129
  96.6 1.7 %norm.1 = bf16[32,128]{1,0:T(8,128)(2,1)} custom-call(bf16[16,32,128]{2,1,0:T(8,128)(2,1)} %all-to-all-done.2.got), custom_call_target="tpu_custom_call" | custom-call | tf_op jit(solution)/shard_map/norm/pallas_call | solution.py:130
  98.3 1.4 %reshape.19 = bf16[3072]{0:T(1024)(128)(2,1)} reshape(bf16[32,96]{1,0:T(8,128)(2,1)} %bitcast.25) | data formatting | bytes 12288 | tf_op jit(solution)/shard_map/reshape | solution.py:133
  99.7 0.0 collective-permute-done.2.refs_2_
  99.7 0.0 collective-permute-done.3.refs_5_
  99.7 0.0 copy-done
  99.7 0.0 copy-done.1
  99.7 0.8 copy-done.4
  100.5 0.8 copy-done.5
  101.3 4.4 %last.1.up_in = bf16[512,3072]{1,0:T(8,128)(2,1)} custom-call(s32[2]{0:T(128)} %pad_add_fusion.pos, bf16[4,288,128]{2,1,0:T(8,128)(2,1)} %copy-done.1, bf16[4,288,128]{2,1,0:T(8,128)(2,1)} %copy-done.3, bf16[2,4,288,128]{3,2,1,0:T(8,128)(2,1)} %copy-done.4, bf16[4,288,128]{2,1,0:T(8,128)(2,1)} %copy-done, bf16[4,288,128]{2,1,0:T(8,128)(2,1)} %copy-done.2, ...), custom_call_target="tpu_custom_call" | custom-call | tf_op jit(solution)/shard_map/last/pallas_call | solution.py:136
  105.7 0.0 all-gather.3.cloned.1.call-done
  105.7 6.9 %first.1 = (bf16[512,3072]{1,0:T(8,128)(2,1)}, bf16[512,3072]{1,0:T(8,128)(2,1)}) custom-call(bf16[8,4,488,128]{3,2,1,0:T(8,128)(2,1)} %bitcast.20, bf16[512,3072]{1,0:T(8,128)(2,1)} %last.1.up_in), custom_call_target="tpu_custom_call", output_to_operand_aliasing={{1}: (1, {})} | custom-call | tf_op jit(solution)/shard_map/first/pallas_call | solution.py:145
  (11 shorter events, 0.0 us)
Async XLA Ops:
  7.2 98.5 %all-gather.3.cloned.1.call-start = ((), (), s32[]{:S(2)}) async-start(), calls=%async_computation.3 | async-start | bytes 4497408 | tf_op jit(solution)/shard_map/all_gather | solution.py:111
  49.9 49.8 %copy-start = (bf16[4,288,128]{2,1,0:T(8,128)(2,1)}, bf16[4,288,128]{2,1,0:T(8,128)(2,1)S(1)}, u32[]{:S(2)}) copy-start(bf16[4,288,128]{2,1,0:T(8,128)(2,1)S(1)} %get-tuple-element.19.refs_3_) | copy-start | bytes 884740
  49.9 49.8 %copy-start.1 = (bf16[4,288,128]{2,1,0:T(8,128)(2,1)}, bf16[4,288,128]{2,1,0:T(8,128)(2,1)S(1)}, u32[]{:S(2)}) copy-start(bf16[4,288,128]{2,1,0:T(8,128)(2,1)S(1)} %get-tuple-element.20.refs_0_) | copy-start | bytes 884740
  49.9 9.1 %collective-permute-start.1 = (bf16[4,288,128]{2,1,0:T(8,128)(2,1)S(1)}, bf16[4,288,128]{2,1,0:T(8,128)(2,1)S(1)}, u32[]{:S(2)}, u32[]{:S(2)}) collective-permute-start(bf16[4,288,128]{2,1,0:T(8,128)(2,1)S(1)} %get-tuple-element.19.refs_3_), channel_id=1, source_target_pairs={{0,48},{16,32},{32,16},{48,0},{64,112},{80,96},{96,80},{112,64},{1... | collective-permute-start | bytes 884744 | tf_op jit(solution)/shard_map/ppermute | solution.py:25
  52.0 7.9 %collective-permute-start = (bf16[4,288,128]{2,1,0:T(8,128)(2,1)S(1)}, bf16[4,288,128]{2,1,0:T(8,128)(2,1)S(1)}, u32[]{:S(2)}, u32[]{:S(2)}) collective-permute-start(bf16[4,288,128]{2,1,0:T(8,128)(2,1)S(1)} %get-tuple-element.20.refs_0_), channel_id=1, source_target_pairs={{0,16},{16,0},{32,48},{48,32},{64,80},{80,64},{96,112},{112,96},{1... | collective-permute-start | bytes 884744 | tf_op jit(solution)/shard_map/ppermute | solution.py:25
  59.0 40.7 %copy-start.2 = (bf16[4,288,128]{2,1,0:T(8,128)(2,1)}, bf16[4,288,128]{2,1,0:T(8,128)(2,1)S(1)}, u32[]{:S(2)}) copy-start(bf16[4,288,128]{2,1,0:T(8,128)(2,1)S(1)} %collective-permute-done.1.refs_4_) | copy-start | bytes 884740
  59.8 39.9 %copy-start.3 = (bf16[4,288,128]{2,1,0:T(8,128)(2,1)}, bf16[4,288,128]{2,1,0:T(8,128)(2,1)S(1)}, u32[]{:S(2)}) copy-start(bf16[4,288,128]{2,1,0:T(8,128)(2,1)S(1)} %collective-permute-done.refs_1_) | copy-start | bytes 884740
  59.9 39.8 %collective-permute-start.2 = (bf16[2,4,288,128]{3,2,1,0:T(8,128)(2,1)S(1)}, bf16[2,4,288,128]{3,2,1,0:T(8,128)(2,1)S(1)}, u32[]{:S(2)}, u32[]{:S(2)}) collective-permute-start(bf16[2,4,288,128]{3,2,1,0:T(8,128)(2,1)S(1)} %pad_maximum_fusion), channel_id=1, source_target_pairs={{0,48},{16,32},{32,16},{48,0},{64,112},{80,96},{96,80},{112,64},{1... | collective-permute-start | bytes 1769480 | tf_op jit(solution)/shard_map/ppermute | solution.py:25
  64.3 35.4 %collective-permute-start.3 = (bf16[2,4,288,128]{3,2,1,0:T(8,128)(2,1)S(1)}, bf16[2,4,288,128]{3,2,1,0:T(8,128)(2,1)S(1)}, u32[]{:S(2)}, u32[]{:S(2)}) collective-permute-start(bf16[2,4,288,128]{3,2,1,0:T(8,128)(2,1)S(1)} %pad_maximum_fusion.1), channel_id=1, source_target_pairs={{0,16},{16,0},{32,48},{48,32},{64,80},{80,64},{96,112},{112,96},{1... | collective-permute-start | bytes 1769480 | tf_op jit(solution)/shard_map/ppermute | solution.py:25
  66.9 29.7 %all-to-all-start.2 = ((bf16[16,32,128]{2,1,0:T(8,128)(2,1)}), bf16[16,32,128]{2,1,0:T(8,128)(2,1)}, u32[]{:S(2)}, u32[]{:S(2)}) async-start(bf16[16,32,128]{2,1,0:T(8,128)(2,1)} %broadcast_in_dim.21), calls=%async_computation.2 | async-start | bytes 262144 | tf_op jit(solution)/shard_map/all_to_all | solution.py:129
  99.7 0.8 copy-start.4
  100.5 0.8 copy-start.5
Sparse Core Ops, SparseCore 0:
  21.1 65.9 all-gather.2

commit v2 on v1

v2 whole, which is shorter than its diff:
```python
import jax
import jax.numpy as jnp
from jax import lax
from jax.experimental import pallas as pl
from jax.experimental.pallas import tpu as pltpu
from jax.sharding import PartitionSpec as P

mix_rate = 1.0
LANES, PIECE = 128, 96
NY, NX, NW = 8, 4, 16
N_FIRST = 6
N_LAST = 8 - N_FIRST
ROWS_FIRST = N_FIRST * PIECE + 8
ROWS_LAST = N_LAST * PIECE
X_ROWS = [[y * NX + x for x in range(NX)] for y in range(NY)]
Y_ROWS = [[y * NX + x for y in range(NY)] for x in range(NX)]


def swap(a, step):
    pairs = []
    for y in range(NY):
        for x in range(NX):
            d = 1 if (x + step) % 2 == 0 else -1
            pairs.append((y * NX + x, y * NX + (x + d) % NX))
    return lax.ppermute(a, "zero", pairs)


def merge_kernel(pos, wg, lg, hg, wu, lu, hu, nt, ns, first, last):
    def whole(w, low_t, high):
        prod = lax.dot_general(low_t[...], high[...], (((0,), (0,)), ((), ())), preferred_element_type=jnp.float32)
        return (w[...].astype(jnp.float32) + mix_rate * prod).astype(jnp.bfloat16)

    gate, up = whole(wg, lg, hg), whole(wu, lu, hu)
    n = (nt[...] + ns[...]).astype(jnp.bfloat16)
    e = lax.broadcasted_iota(jnp.int32, (6, LANES), 0)
    eye = (e + pos[2] == lax.broadcasted_iota(jnp.int32, (6, LANES), 1)).astype(jnp.bfloat16)
    rows = jnp.dot(jnp.broadcast_to(n, (8, 6)), eye, preferred_element_type=jnp.float32).astype(jnp.bfloat16)
    for t in range(8):
        c = (t % 4) * LANES
        tile = (gate if t < 4 else up)[:, c:c + LANES]
        if t < N_FIRST:
            for x in range(NX):
                first[x, t * PIECE:(t + 1) * PIECE, :] = tile
        else:
            last[(t - N_FIRST) * PIECE:(t - N_FIRST + 1) * PIECE, :] = tile
    for x in range(NX):
        first[x, N_FIRST * PIECE:, :] = rows


def assemble(fetch, tiles, outs, buf, stage, sem_out):
    stores = []
    for y in range(NY):
        for cp in fetch[y]:
            cp.wait()
        for t in range(tiles):
            block = jnp.concatenate([buf[y, x, t * PIECE:(t + 1) * PIECE, :] for x in range(NX)], axis=0)
            stage[y, t * LANES:(t + 1) * LANES, :] = block.T
        for k, (out, at, row, rows) in enumerate(outs):
            cp = pltpu.make_async_copy(
                stage.at[y, pl.ds(at, rows), :], out.at[pl.ds(row, rows), pl.ds(y * 384, 384)], sem_out.at[k, y])
            cp.start()
            stores.append(cp)
    for cp in stores:
        cp.wait()


def last_kernel(pos, *refs):
    ins, (up, buf, stage, sem_in, sem_out) = refs[:6], refs[6:]
    fetch = []
    for y in range(NY):
        h, g = divmod(y, NY // 2)
        own, near, far = ins[3 * h:3 * h + 3]
        s = pos[1] if h == 0 else -pos[1]
        parts = ((own.at[g], 0), (near.at[g], 1), (far.at[0, g], -1), (far.at[1, g], -2))
        fetch.append([
            pltpu.make_async_copy(part, buf.at[y, (pos[0] + m * s + NX) & (NX - 1)], sem_in.at[y, k])
            for k, (part, m) in enumerate(parts)
        ])
        for cp in fetch[-1]:
            cp.start()
    n = N_LAST * LANES
    assemble(fetch, N_LAST, [(up, 0, 512 - n, n)], buf, stage, sem_out)


def first_kernel(got, up_in, gate, up, buf, stage, sem_in, sem_out):
    fetch = [[pltpu.make_async_copy(got.at[y], buf.at[y], sem_in.at[y])] for y in range(NY)]
    for cps in fetch:
        cps[0].start()
    n = (N_FIRST - 4) * LANES
    assemble(fetch, N_FIRST, [(gate, 0, 0, 512), (up, 512, 0, n)], buf, stage, sem_out)


def norm_kernel(got, out):
    total = jnp.zeros((32, LANES), jnp.float32)
    i = lax.broadcasted_iota(jnp.int32, (32, LANES), 0)
    lane = lax.broadcasted_iota(jnp.int32, (32, LANES), 1)
    at = lane - 6 * (i & 15)
    own = (at >= 0) & (at < 6)
    e = lax.broadcasted_iota(jnp.int32, (LANES, LANES), 0) % 6
    c = lax.broadcasted_iota(jnp.int32, (LANES, LANES), 1)
    for j in range(NW):
        r = got[j].astype(jnp.float32)
        rows = jnp.where(i < 16, jnp.broadcast_to(r[0:1], (32, LANES)), jnp.broadcast_to(r[1:2], (32, LANES)))
        rows = jnp.where(own, rows, 0.0).astype(jnp.bfloat16)
        total += jnp.dot(rows, (c == e + 6 * j).astype(jnp.bfloat16), preferred_element_type=jnp.float32)
    out[...] = total.astype(jnp.bfloat16)


def on_device(w_gate, low_gate, high_gate, w_up, low_up, high_up, norm_train, norm_step):
    vm = pl.BlockSpec(memory_space=pltpu.VMEM)
    sm = pl.BlockSpec(memory_space=pltpu.SMEM)
    hb = pl.BlockSpec(memory_space=pl.ANY)
    bf16 = jnp.bfloat16
    zero = lax.axis_index("zero")
    x = zero & (NX - 1)
    pos = jnp.stack([x, 1 - 2 * (x & 1), 6 * (zero & 15)]).astype(jnp.int32)
    first, last = pl.pallas_call(
        merge_kernel, in_specs=[sm] + [vm] * 8, out_specs=[vm, vm],
        out_shape=[jax.ShapeDtypeStruct((NX, ROWS_FIRST, LANES), bf16), jax.ShapeDtypeStruct((ROWS_LAST, LANES), bf16)],
        name="merge",
    )(pos, w_gate, low_gate.T, high_gate, w_up, low_up.T, high_up, norm_train[None, :], norm_step[None, :])

    along_x = lax.all_to_all(first, "zero", 0, 0, tiled=True, axis_index_groups=X_ROWS)
    got_first = lax.all_gather(along_x, "zero", axis=0, axis_index_groups=Y_ROWS)

    norm_x = jnp.sum(along_x[:, N_FIRST * PIECE:, :].astype(jnp.float32), axis=0).astype(bf16)
    own = jnp.concatenate([last, norm_x], axis=0)
    along_y = lax.all_to_all(
        jnp.broadcast_to(own[None], (NY,) + own.shape), "zero", 0, 0, tiled=True, axis_index_groups=Y_ROWS)

    halves = []
    for h in range(2):
        a = along_y[h * 4:(h + 1) * 4, :ROWS_LAST]
        halves.append((a, swap(a, h)))
    norm_y = along_y[:, ROWS_LAST:].astype(jnp.float32).reshape(2, 4, 8, LANES)
    norm_rows = jnp.sum(norm_y, axis=1)[:, 0, :]
    norm_rows = jnp.concatenate([norm_rows, jnp.zeros((6, LANES), jnp.float32)], axis=0).astype(bf16)
    both = [jnp.stack(h) for h in halves]
    *both, norm_rows = lax.optimization_barrier((*both, norm_rows))
    parts = []
    for h in range(2):
        parts += [*halves[h], swap(both[h], 1 - h)]

    spread = lax.all_to_all(jnp.broadcast_to(norm_rows[None], (NW, 8, LANES)), "width", 0, 0, tiled=True)
    norm = pl.pallas_call(
        norm_kernel, in_specs=[vm], out_specs=vm, out_shape=jax.ShapeDtypeStruct((32, LANES), bf16), name="norm",
    )(spread)
    serve_norm = norm[:, :PIECE].reshape(3072)

    out = jax.ShapeDtypeStruct((512, 3072), bf16)

    def scratch(rows, tiles, n_out, sem_in):
        return [
            pltpu.VMEM((NY, NX, rows, LANES), bf16),
            pltpu.VMEM((NY, tiles * LANES, 384), bf16),
            pltpu.SemaphoreType.DMA(sem_in),
            pltpu.SemaphoreType.DMA((n_out, NY)),
        ]

    up = pl.pallas_call(
        last_kernel, in_specs=[sm] + [hb] * 6, out_specs=hb, out_shape=out,
        scratch_shapes=scratch(ROWS_LAST, N_LAST, 1, (NY, NX)), name="last",
    )(pos, *parts)
    gate, up = pl.pallas_call(
        first_kernel, in_specs=[hb, hb], out_specs=[hb, hb], out_shape=[out, out],
        scratch_shapes=scratch(ROWS_FIRST, N_FIRST, 2, (NY,)), input_output_aliases={1: 1}, name="first",
    )(got_first, up)
    return (gate, up, serve_norm)


def solution(mesh):
    placed = (
        P("zero", "width"), P("zero", None), P(None, "width"),
        P("zero", "width"), P("zero", None), P(None, "width"),
        P(("zero", "width")), P(("zero", "width")),
    )
    return jax.shard_map(
        on_device, mesh=mesh, in_specs=placed,
        out_specs=(P("width", None), P("width", None), P()), check_vma=False,
    )
```

time: 120 us -> 106 us (0.88)
  blocking collectives: 38.8 us -> 60.1 us
  starting transfers between devices: 31.1 us -> 10.4 us
  waiting for transfers between devices: 14.2 us -> 4.83 us
  Pallas kernels: 15 us -> 11.1 us
  local copies, waits for them, and re-layouts: 4.62 us -> 3.03 us
    all_to_all x0 -> x1, blocking collectives: none -> 26.4 us  [on_device(): lax.all_to_all(jnp.broadcast_to(norm_rows[None], (NW, 8, LANES)), 'width'...]
    all_to_all x1 -> x0, starting transfers between devices: 20.7 us -> none  [on_device(): lax.all_to_all(jnp.broadcast_to(norm_rows[None], (NW, 32, LANES)), 'width...]
    all_to_all x1 -> x0, waiting for transfers between devices: 8.35 us -> none  [on_device(): lax.all_to_all(jnp.broadcast_to(norm_rows[None], (NW, 32, LANES)), 'width...]
    all_to_all x1, blocking collectives: 27 us -> 21.4 us  [on_device(): lax.all_to_all(jnp.broadcast_to(own[None], (NY,) + own.shape), 'zero', 0,...]
    pallas_call x3, Pallas kernels: 13.3 us -> 9.45 us  [the longest x1 3.93 us: on_device(): pl.pallas_call(first_kernel, in_specs=[hb, hb], out_specs=[hb, hb], out_s...]
  transfers between devices with their start and end apart: 6 -> 5, of which waited for: 3 -> 2; matrix products, arithmetic and copies ran while one was open for 4% -> 3% of each run, Pallas kernels for 5% -> 5%
where the time goes in v2:
time: 106 us
  blocking collectives  60.1 us (57%)
  between operations  14.2 us (13%)
  Pallas kernels  11.1 us (10%)
  starting transfers between devices  10.4 us (10%)
  waiting for transfers between devices  4.83 us (5%)
  local copies, waits for them, and re-layouts  3.03 us (3%)
  other arithmetic  2.19 us (2%)
    all_to_all x1, blocking collectives, on_device(): lax.all_to_all(jnp.broadcast_to(norm_rows[None], (NW, 8, LANES)), 'width'...  26.4 us
    all_to_all x1, blocking collectives, on_device(): lax.all_to_all(jnp.broadcast_to(own[None], (NY,) + own.shape), 'zero', 0,...  21.4 us
    all_to_all x1, blocking collectives, on_device(): lax.all_to_all(first, 'zero', 0, 0, tiled=True, axis_index_groups=X_ROWS)  12.3 us
    ppermute x4, starting transfers between devices, swap(): return lax.ppermute(a, 'zero', pairs)  10.3 us
    ppermute x4, waiting for transfers between devices, swap(): return lax.ppermute(a, 'zero', pairs)  4.8 us
    pallas_call x1, Pallas kernels, on_device(): pl.pallas_call(first_kernel, in_specs=[hb, hb], out_specs=[hb, hb], out_s...  3.93 us
    pallas_call x1, Pallas kernels, on_device(): pl.pallas_call(last_kernel, in_specs=[sm] + [hb] * 6, out_specs=hb, out_s...  3.45 us
  transfers between devices with their start and end apart: 5, of which 2 were waited for; matrix products, arithmetic and copies ran while one was open for 3% of the time, Pallas kernels for 5%

profile of v2, /device:TPU:1, one launch (start us, length us, event | category | flops | bytes accessed | tf_op | source)
XLA Modules:
  0.0 105.8 jit_solution(11056459857568028375)
XLA Ops:
  7.2 0.0 all-gather.3.cloned.1.call-start
  7.2 0.6 pad_add_fusion.pos
  7.8 2.1 %merge.1 = (bf16[4,584,128]{2,1,0:T(8,128)(2,1)}, bf16[192,128]{1,0:T(8,128)(2,1)}) custom-call(s32[3]{0:T(128)} %pad_add_fusion.pos, bf16[96,512]{1,0:T(8,128)(2,1)} %wg.1, bf16[16,96]{1,0:T(8,128)(2,1)} %bitcast.24, bf16[16,512]{1,0:T(8,128)(2,1)} %hg.1, bf16[96,512]{1,0:T(8,128)(2,1)} %wu.1, bf16[16,96]{1,0:T(8,128)(2,1)} %bitcast.25, ...), custom_call_target="tpu_custom_call" | custom-call | tf_op jit(solution)/shard_map/merge/pallas_call | solution.py:117
  9.9 12.3 %all_to_all.15 = bf16[4,584,128]{2,1,0:T(8,128)(2,1)} all-to-all(bf16[4,584,128]{2,1,0:T(8,128)(2,1)} %get-tuple-element.10), channel_id=1, replica_groups={{0,16,32,48},{64,80,96,112},{128,144,160,176},{192,208,224,240},{256,27..., dimensions={0} | all-to-all | bytes 1196032 | tf_op jit(solution)/shard_map/all_to_all | solution.py:123
  22.1 0.0 all-gather.3.cloned.1.call-update
  22.2 0.7 slice_reduce_fusion
  22.9 0.8 pad_maximum_fusion.2
  23.7 0.1 broadcast_in_dim.10
  23.7 21.4 %all_to_all.16 = bf16[8,200,128]{2,1,0:T(8,128)(2,1)S(1)} all-to-all(bf16[8,200,128]{2,1,0:T(8,128)(2,1)S(1)} %broadcast_in_dim.10), channel_id=1, replica_groups={{0,64,128,192,256,320,384,448},{16,80,144,208,272,336,400,464},{32,96,1..., dimensions={0} | all-to-all | bytes 819200 | tf_op jit(solution)/shard_map/all_to_all | solution.py:128
  45.2 0.1 slice_bitcast_fusion
  45.3 0.0 copy-start
  45.3 0.0 copy-start.1
  45.3 2.8 %collective-permute-start.1 = (bf16[4,192,128]{2,1,0:T(8,128)(2,1)S(1)}, bf16[4,192,128]{2,1,0:T(8,128)(2,1)S(1)}, u32[]{:S(2)}, u32[]{:S(2)}) collective-permute-start(bf16[4,192,128]{2,1,0:T(8,128)(2,1)S(1)} %get-tuple-element.19.refs_3_), channel_id=1, source_target_pairs={{0,48},{16,32},{32,16},{48,0},{64,112},{80,96},{96,80},{112,64},{1... | collective-permute-start | bytes 589832 | tf_op jit(solution)/shard_map/ppermute | solution.py:25
  48.1 1.9 %collective-permute-start = (bf16[4,192,128]{2,1,0:T(8,128)(2,1)S(1)}, bf16[4,192,128]{2,1,0:T(8,128)(2,1)S(1)}, u32[]{:S(2)}, u32[]{:S(2)}) collective-permute-start(bf16[4,192,128]{2,1,0:T(8,128)(2,1)S(1)} %get-tuple-element.20.refs_0_), channel_id=1, source_target_pairs={{0,16},{16,0},{32,48},{48,32},{64,80},{80,64},{96,112},{112,96},{1... | collective-permute-start | bytes 589832 | tf_op jit(solution)/shard_map/ppermute | solution.py:25
  50.1 3.2 %collective-permute-done.1.refs_4_ = bf16[4,192,128]{2,1,0:T(8,128)(2,1)S(1)} collective-permute-done((bf16[4,192,128]{2,1,0:T(8,128)(2,1)S(1)}, bf16[4,192,128]{2,1,0:T(8,128)(2,1)S(1)}, u32[]{:S(2)}, u32[]{:S(2)}) %collective-permute-start.1) | collective-permute-done | bytes 196640 | tf_op jit(solution)/shard_map/ppermute | solution.py:25
  53.4 1.5 %collective-permute-done.refs_1_ = bf16[4,192,128]{2,1,0:T(8,128)(2,1)S(1)} collective-permute-done((bf16[4,192,128]{2,1,0:T(8,128)(2,1)S(1)}, bf16[4,192,128]{2,1,0:T(8,128)(2,1)S(1)}, u32[]{:S(2)}, u32[]{:S(2)}) %collective-permute-start) | collective-permute-done | bytes 196640 | tf_op jit(solution)/shard_map/ppermute | solution.py:25
  55.0 3.7 %collective-permute-start.2 = (bf16[2,4,192,128]{3,2,1,0:T(8,128)(2,1)S(1)}, bf16[2,4,192,128]{3,2,1,0:T(8,128)(2,1)S(1)}, u32[]{:S(2)}, u32[]{:S(2)}) collective-permute-start(bf16[2,4,192,128]{3,2,1,0:T(8,128)(2,1)S(1)} %pad_maximum_fusion), channel_id=1, source_target_pairs={{0,48},{16,32},{32,16},{48,0},{64,112},{80,96},{96,80},{112,64},{1... | collective-permute-start | bytes 1179656 | tf_op jit(solution)/shard_map/ppermute | solution.py:25
  58.7 1.9 %collective-permute-start.3 = (bf16[2,4,192,128]{3,2,1,0:T(8,128)(2,1)S(1)}, bf16[2,4,192,128]{3,2,1,0:T(8,128)(2,1)S(1)}, u32[]{:S(2)}, u32[]{:S(2)}) collective-permute-start(bf16[2,4,192,128]{3,2,1,0:T(8,128)(2,1)S(1)} %pad_maximum_fusion.1), channel_id=1, source_target_pairs={{0,16},{16,0},{32,48},{48,32},{64,80},{80,64},{96,112},{112,96},{1... | collective-permute-start | bytes 1179656 | tf_op jit(solution)/shard_map/ppermute | solution.py:25
  60.6 26.4 %all_to_all.17.got = bf16[16,8,128]{2,1,0:T(8,128)(2,1)} all-to-all(bf16[16,8,128]{2,1,0:T(8,128)(2,1)S(1)} %broadcast_in_dim.22), channel_id=1, replica_groups=mesh['zero'=32,'width'=16] {'width'}, dimensions={0} | all-to-all | bytes 65536 | tf_op jit(solution)/shard_map/all_to_all | solution.py:144
  87.0 1.6 %norm.1 = bf16[32,128]{1,0:T(8,128)(2,1)} custom-call(bf16[16,8,128]{2,1,0:T(8,128)(2,1)} %all_to_all.17.got), custom_call_target="tpu_custom_call" | custom-call | tf_op jit(solution)/shard_map/norm/pallas_call | solution.py:145
  88.6 1.4 %reshape.19 = bf16[3072]{0:T(1024)(128)(2,1)} reshape(bf16[32,96]{1,0:T(8,128)(2,1)} %bitcast.23) | data formatting | bytes 12288 | tf_op jit(solution)/shard_map/reshape | solution.py:148
  90.0 0.0 collective-permute-done.2.refs_2_
  90.0 0.0 collective-permute-done.3.refs_5_
  90.0 0.0 copy-done
  90.0 0.0 copy-done.1
  90.0 0.0 copy-done.2
  90.0 0.0 copy-done.3
  90.0 0.7 copy-done.4
  90.7 0.8 copy-done.5
  91.5 3.5 %last.1.up_in = bf16[512,3072]{1,0:T(8,128)(2,1)} custom-call(s32[3]{0:T(128)} %pad_add_fusion.pos, bf16[4,192,128]{2,1,0:T(8,128)(2,1)} %copy-done.1, bf16[4,192,128]{2,1,0:T(8,128)(2,1)} %copy-done.3, bf16[2,4,192,128]{3,2,1,0:T(8,128)(2,1)} %copy-done.4, bf16[4,192,128]{2,1,0:T(8,128)(2,1)} %copy-done, bf16[4,192,128]{2,1,0:T(8,128)(2,1)} %copy-done.2, ...), custom_call_target="tpu_custom_call" | custom-call | tf_op jit(solution)/shard_map/last/pallas_call | solution.py:160
  94.9 0.0 all-gather.3.cloned.1.call-done
  95.0 3.9 %first.1 = (bf16[512,3072]{1,0:T(8,128)(2,1)}, bf16[512,3072]{1,0:T(8,128)(2,1)}) custom-call(bf16[8,4,584,128]{3,2,1,0:T(8,128)(2,1)} %bitcast.20, bf16[512,3072]{1,0:T(8,128)(2,1)} %last.1.up_in), custom_call_target="tpu_custom_call", output_to_operand_aliasing={{1}: (1, {})} | custom-call | tf_op jit(solution)/shard_map/first/pallas_call | solution.py:164
  (11 shorter events, 0.1 us)
Async XLA Ops:
  7.2 87.8 %all-gather.3.cloned.1.call-start = ((), (), s32[]{:S(2)}) async-start(), calls=%async_computation.3 | async-start | bytes 5382144 | tf_op jit(solution)/shard_map/all_gather | solution.py:124
  45.3 44.7 %copy-start = (bf16[4,192,128]{2,1,0:T(8,128)(2,1)}, bf16[4,192,128]{2,1,0:T(8,128)(2,1)S(1)}, u32[]{:S(2)}) copy-start(bf16[4,192,128]{2,1,0:T(8,128)(2,1)S(1)} %get-tuple-element.19.refs_3_) | copy-start | bytes 589828
  45.3 44.7 %copy-start.1 = (bf16[4,192,128]{2,1,0:T(8,128)(2,1)}, bf16[4,192,128]{2,1,0:T(8,128)(2,1)S(1)}, u32[]{:S(2)}) copy-start(bf16[4,192,128]{2,1,0:T(8,128)(2,1)S(1)} %get-tuple-element.20.refs_0_) | copy-start | bytes 589828
  45.3 8.0 %collective-permute-start.1 = (bf16[4,192,128]{2,1,0:T(8,128)(2,1)S(1)}, bf16[4,192,128]{2,1,0:T(8,128)(2,1)S(1)}, u32[]{:S(2)}, u32[]{:S(2)}) collective-permute-start(bf16[4,192,128]{2,1,0:T(8,128)(2,1)S(1)} %get-tuple-element.19.refs_3_), channel_id=1, source_target_pairs={{0,48},{16,32},{32,16},{48,0},{64,112},{80,96},{96,80},{112,64},{1... | collective-permute-start | bytes 589832 | tf_op jit(solution)/shard_map/ppermute | solution.py:25
  48.1 6.8 %collective-permute-start = (bf16[4,192,128]{2,1,0:T(8,128)(2,1)S(1)}, bf16[4,192,128]{2,1,0:T(8,128)(2,1)S(1)}, u32[]{:S(2)}, u32[]{:S(2)}) collective-permute-start(bf16[4,192,128]{2,1,0:T(8,128)(2,1)S(1)} %get-tuple-element.20.refs_0_), channel_id=1, source_target_pairs={{0,16},{16,0},{32,48},{48,32},{64,80},{80,64},{96,112},{112,96},{1... | collective-permute-start | bytes 589832 | tf_op jit(solution)/shard_map/ppermute | solution.py:25
  53.3 36.7 %copy-start.2 = (bf16[4,192,128]{2,1,0:T(8,128)(2,1)}, bf16[4,192,128]{2,1,0:T(8,128)(2,1)S(1)}, u32[]{:S(2)}) copy-start(bf16[4,192,128]{2,1,0:T(8,128)(2,1)S(1)} %collective-permute-done.1.refs_4_) | copy-start | bytes 589828
  54.9 35.1 %copy-start.3 = (bf16[4,192,128]{2,1,0:T(8,128)(2,1)}, bf16[4,192,128]{2,1,0:T(8,128)(2,1)S(1)}, u32[]{:S(2)}) copy-start(bf16[4,192,128]{2,1,0:T(8,128)(2,1)S(1)} %collective-permute-done.refs_1_) | copy-start | bytes 589828
  55.0 35.0 %collective-permute-start.2 = (bf16[2,4,192,128]{3,2,1,0:T(8,128)(2,1)S(1)}, bf16[2,4,192,128]{3,2,1,0:T(8,128)(2,1)S(1)}, u32[]{:S(2)}, u32[]{:S(2)}) collective-permute-start(bf16[2,4,192,128]{3,2,1,0:T(8,128)(2,1)S(1)} %pad_maximum_fusion), channel_id=1, source_target_pairs={{0,48},{16,32},{32,16},{48,0},{64,112},{80,96},{96,80},{112,64},{1... | collective-permute-start | bytes 1179656 | tf_op jit(solution)/shard_map/ppermute | solution.py:25
  58.7 31.3 %collective-permute-start.3 = (bf16[2,4,192,128]{3,2,1,0:T(8,128)(2,1)S(1)}, bf16[2,4,192,128]{3,2,1,0:T(8,128)(2,1)S(1)}, u32[]{:S(2)}, u32[]{:S(2)}) collective-permute-start(bf16[2,4,192,128]{3,2,1,0:T(8,128)(2,1)S(1)} %pad_maximum_fusion.1), channel_id=1, source_target_pairs={{0,16},{16,0},{32,48},{48,32},{64,80},{80,64},{96,112},{112,96},{1... | collective-permute-start | bytes 1179656 | tf_op jit(solution)/shard_map/ppermute | solution.py:25
  90.0 0.7 copy-start.4
  90.7 0.8 copy-start.5
Sparse Core Ops, SparseCore 0:
  22.3 69.2 all-gather.2

commit v3 on v2

v3 whole, which is shorter than its diff:
```python
import jax
import jax.numpy as jnp
from jax import lax
from jax.experimental import pallas as pl
from jax.experimental.pallas import tpu as pltpu
from jax.sharding import PartitionSpec as P


mix_rate = 1.0
LANES, PIECE = 128, 96
NY, NX, NW = 8, 4, 16
N_FIRST = 6
N_LAST = 8 - N_FIRST
ROWS_FIRST = N_FIRST * PIECE + 8
ROWS_LAST = N_LAST * PIECE
X_ROWS = [[y * NX + x for x in range(NX)] for y in range(NY)]
Y_ROWS = [[y * NX + x for y in range(NY)] for x in range(NX)]


def swap(a, step):
    pairs = []
    for y in range(NY):
        for x in range(NX):
            d = 1 if (x + step) % 2 == 0 else -1
            pairs.append((y * NX + x, y * NX + (x + d) % NX))
    return lax.ppermute(a, "zero", pairs)


def merge_kernel(wg, lg, hg, wu, lu, hu, nt, ns, first, last):
    def whole(w, low_t, high):
        prod = lax.dot_general(low_t[...], high[...], (((0,), (0,)), ((), ())), preferred_element_type=jnp.float32)
        return (w[...].astype(jnp.float32) + mix_rate * prod).astype(jnp.bfloat16)

    gate, up = whole(wg, lg, hg), whole(wu, lu, hu)
    at = 96 * (lax.axis_index("zero") & (NX - 1)) + 6 * lax.axis_index("width")
    n = jnp.broadcast_to((nt[...] + ns[...]).astype(jnp.bfloat16), (8, 6))
    e = lax.broadcasted_iota(jnp.int32, (6, LANES), 0)
    lane = lax.broadcasted_iota(jnp.int32, (6, LANES), 1)
    row = lax.broadcasted_iota(jnp.int32, (8, LANES), 0)
    rows = jnp.zeros((8, LANES), jnp.float32)
    for r in range(3):
        eye = (e + at == lane + r * LANES).astype(jnp.bfloat16)
        rows = jnp.where(row == r, jnp.dot(n, eye, preferred_element_type=jnp.float32), rows)
    rows = rows.astype(jnp.bfloat16)
    for t in range(8):
        c = (t % 4) * LANES
        tile = (gate if t < 4 else up)[:, c:c + LANES]
        if t < N_FIRST:
            for x in range(NX):
                first[x, t * PIECE:(t + 1) * PIECE, :] = tile
        else:
            last[(t - N_FIRST) * PIECE:(t - N_FIRST + 1) * PIECE, :] = tile
    for x in range(NX):
        first[x, N_FIRST * PIECE:, :] = rows


def assemble(fetch, tiles, outs, buf, stage, sem_out):
    stores = []
    for y in range(NY):
        for cp in fetch[y]:
            cp.wait()
        for t in range(tiles):
            block = jnp.concatenate([buf[y, x, t * PIECE:(t + 1) * PIECE, :] for x in range(NX)], axis=0)
            stage[y, t * LANES:(t + 1) * LANES, :] = block.T
        for k, (out, at, row, rows) in enumerate(outs):
            cp = pltpu.make_async_copy(
                stage.at[y, pl.ds(at, rows), :], out.at[pl.ds(row, rows), pl.ds(y * 384, 384)], sem_out.at[k, y])
            cp.start()
            stores.append(cp)
    for cp in stores:
        cp.wait()


def last_kernel(*refs):
    x = lax.axis_index("zero") & (NX - 1)
    ins, (up, buf, stage, sem_in, sem_out) = refs[:6], refs[6:]
    fetch = []
    for y in range(NY):
        h, g = divmod(y, NY // 2)
        own, near, far = ins[3 * h:3 * h + 3]
        s = (1 - 2 * (x & 1)) * (1 - 2 * h)
        parts = ((own.at[g], 0), (near.at[g], 1), (far.at[0, g], -1), (far.at[1, g], -2))
        fetch.append([
            pltpu.make_async_copy(part, buf.at[y, (x + m * s + NX) & (NX - 1)], sem_in.at[y, k])
            for k, (part, m) in enumerate(parts)
        ])
        for cp in fetch[-1]:
            cp.start()
    n = N_LAST * LANES
    assemble(fetch, N_LAST, [(up, 0, 512 - n, n)], buf, stage, sem_out)


def first_kernel(got, up_in, gate, up, buf, stage, sem_in, sem_out):
    fetch = [[pltpu.make_async_copy(got.at[y], buf.at[y], sem_in.at[y])] for y in range(NY)]
    for cps in fetch:
        cps[0].start()
    n = (N_FIRST - 4) * LANES
    assemble(fetch, N_FIRST, [(gate, 0, 0, 512), (up, 512, 0, n)], buf, stage, sem_out)


def program(w_gate, low_gate, high_gate, w_up, low_up, high_up, norm_train, norm_step):
    vm = pl.BlockSpec(memory_space=pltpu.VMEM)
    hb = pl.BlockSpec(memory_space=pl.ANY)
    bf16 = jnp.bfloat16
    first, last = pl.pallas_call(
        merge_kernel, in_specs=[vm] * 8, out_specs=[vm, vm],
        out_shape=[jax.ShapeDtypeStruct((NX, ROWS_FIRST, LANES), bf16), jax.ShapeDtypeStruct((ROWS_LAST, LANES), bf16)],
        name="merge",
    )(w_gate, low_gate.T, high_gate, w_up, low_up.T, high_up, norm_train[None, :], norm_step[None, :])

    along_x = lax.all_to_all(first, "zero", 0, 0, tiled=True, axis_index_groups=X_ROWS)
    got_first = lax.all_gather(along_x, "zero", axis=0, axis_index_groups=Y_ROWS)

    norm_x = jnp.sum(along_x[:, N_FIRST * PIECE:, :].astype(jnp.float32), axis=0).astype(bf16)
    own = jnp.concatenate([last, norm_x], axis=0)
    along_y = lax.all_to_all(
        jnp.broadcast_to(own[None], (NY,) + own.shape), "zero", 0, 0, tiled=True, axis_index_groups=Y_ROWS)

    norm_xy = along_y[:, ROWS_LAST:ROWS_LAST + 3].reshape(24, LANES)
    spread = lax.all_to_all(jnp.broadcast_to(norm_xy[None], (NW, 24, LANES)), "width", 0, 0, tiled=True)
    serve_norm = jnp.sum(spread.astype(jnp.float32), axis=0).astype(bf16).reshape(3072)

    halves = []
    for h in range(2):
        a = along_y[h * 4:(h + 1) * 4, :ROWS_LAST]
        halves.append((a, swap(a, h)))
    both = [jnp.concatenate([a[None], b[None]], axis=0) for a, b in halves]
    parts = []
    for h in range(2):
        parts += [*halves[h], swap(both[h], 1 - h)]

    out = jax.ShapeDtypeStruct((512, 3072), bf16)

    def scratch(rows, tiles, n_out, sem_in):
        return [
            pltpu.VMEM((NY, NX, rows, LANES), bf16),
            pltpu.VMEM((NY, tiles * LANES, 384), bf16),
            pltpu.SemaphoreType.DMA(sem_in),
            pltpu.SemaphoreType.DMA((n_out, NY)),
        ]

    up = pl.pallas_call(
        last_kernel, in_specs=[hb] * 6, out_specs=hb, out_shape=out,
        scratch_shapes=scratch(ROWS_LAST, N_LAST, 1, (NY, NX)), name="last",
    )(*parts)
    gate, up = pl.pallas_call(
        first_kernel, in_specs=[hb, hb], out_specs=[hb, hb], out_shape=[out, out],
        scratch_shapes=scratch(ROWS_FIRST, N_FIRST, 2, (NY,)), input_output_aliases={1: 1}, name="first",
    )(got_first, up)
    return (gate, up, serve_norm)


def solution(mesh):
    placed = (
        P("zero", "width"), P("zero", None), P(None, "width"),
        P("zero", "width"), P("zero", None), P(None, "width"),
        P(("zero", "width")), P(("zero", "width")),
    )
    return jax.shard_map(
        program, mesh=mesh, in_specs=placed,
        out_specs=(P("width", None), P("width", None), P()), check_vma=False,
    )
```

time: 106 us -> 102 us (0.962)
  Pallas kernels: 11.1 us -> 8.76 us
  blocking collectives: 60.1 us -> 62.1 us
  waiting for transfers between devices: 4.83 us -> 3.41 us
  local copies, waits for them, and re-layouts: 3.03 us -> 1.68 us
    pallas_call x4 -> x3, Pallas kernels: 11.1 us -> 8.76 us  [the longest x1 3.93 us: program(): pl.pallas_call(first_kernel, in_specs=[hb, hb], out_specs=[hb, hb], out_s...]
    ppermute x4, waiting for transfers between devices: 4.8 us -> 2.7 us  [swap(): return lax.ppermute(a, 'zero', pairs)]
    all_to_all x3, blocking collectives: 60.1 us -> 62.1 us  [the longest x1 28.4 us: program(): lax.all_to_all(jnp.broadcast_to(norm_xy[None], (NW, 24, LANES)), 'width',...]
    reshape x1 -> x0, local copies, waits for them, and re-layouts: 1.37 us -> none  [on_device(): serve_norm = norm[:, :PIECE].reshape(3072)]
  transfers between devices with their start and end apart: 5 -> 5, of which waited for: 2 -> 3; matrix products, arithmetic and copies ran while one was open for 3% -> 2% of each run, Pallas kernels for 5% -> 3%
where the time goes in v3:
time: 102 us
  blocking collectives  62.1 us (61%)
  between operations  14.2 us (14%)
  starting transfers between devices  9.42 us (9%)
  Pallas kernels  8.76 us (9%)
  waiting for transfers between devices  3.41 us (3%)
  other arithmetic  2.2 us (2%)
  local copies, waits for them, and re-layouts  1.68 us (2%)
    all_to_all x1, blocking collectives, program(): lax.all_to_all(jnp.broadcast_to(norm_xy[None], (NW, 24, LANES)), 'width',...  28.4 us
    all_to_all x1, blocking collectives, program(): lax.all_to_all(jnp.broadcast_to(own[None], (NY,) + own.shape), 'zero', 0,...  21.5 us
    all_to_all x1, blocking collectives, program(): lax.all_to_all(first, 'zero', 0, 0, tiled=True, axis_index_groups=X_ROWS)  12.3 us
    ppermute x4, starting transfers between devices, swap(): return lax.ppermute(a, 'zero', pairs)  9.39 us
    pallas_call x1, Pallas kernels, program(): pl.pallas_call(first_kernel, in_specs=[hb, hb], out_specs=[hb, hb], out_s...  3.93 us
    pallas_call x1, Pallas kernels, program(): pl.pallas_call(last_kernel, in_specs=[hb] * 6, out_specs=hb, out_shape=ou...  2.78 us
    ppermute x4, waiting for transfers between devices, swap(): return lax.ppermute(a, 'zero', pairs)  2.7 us
    pallas_call x1, Pallas kernels, program(): pl.pallas_call(merge_kernel, in_specs=[vm] * 8, out_specs=[vm, vm], out_s...  2.05 us
  transfers between devices with their start and end apart: 5, of which 3 were waited for; matrix products, arithmetic and copies ran while one was open for 2% of the time, Pallas kernels for 3%

profile of v3, /device:TPU:1, one launch (start us, length us, event | category | flops | bytes accessed | tf_op | source)
XLA Modules:
  0.0 101.7 jit_solution(4119633989980507316)
XLA Ops:
  7.2 0.0 all-gather.3.cloned.1.call-start
  7.2 2.1 %merge.1 = (bf16[4,584,128]{2,1,0:T(8,128)(2,1)}, bf16[192,128]{1,0:T(8,128)(2,1)}) custom-call(bf16[96,512]{1,0:T(8,128)(2,1)} %wg.1, bf16[16,96]{1,0:T(8,128)(2,1)} %bitcast.16, bf16[16,512]{1,0:T(8,128)(2,1)} %hg.1, bf16[96,512]{1,0:T(8,128)(2,1)} %wu.1, bf16[16,96]{1,0:T(8,128)(2,1)} %bitcast.17, bf16[16,512]{1,0:T(8,128)(2,1)} %hu.1, f32[1,6]{1,0:T(1,128)} %bitcast.18, ...), custom_call_target="tpu_custom_call" | custom-call | tf_op jit(solution)/shard_map/merge/pallas_call | solution.py:105
  9.3 12.3 %all_to_all.15 = bf16[4,584,128]{2,1,0:T(8,128)(2,1)} all-to-all(bf16[4,584,128]{2,1,0:T(8,128)(2,1)} %get-tuple-element.7), channel_id=1, replica_groups={{0,16,32,48},{64,80,96,112},{128,144,160,176},{192,208,224,240},{256,27..., dimensions={0} | all-to-all | bytes 1196032 | tf_op jit(solution)/shard_map/all_to_all | solution.py:111
  21.5 0.0 all-gather.3.cloned.1.call-update
  21.6 0.7 slice_reduce_fusion
  22.3 0.8 pad_maximum_fusion.2
  23.1 0.1 broadcast_in_dim.33
  23.1 21.5 %all_to_all.16 = bf16[8,200,128]{2,1,0:T(8,128)(2,1)S(1)} all-to-all(bf16[8,200,128]{2,1,0:T(8,128)(2,1)S(1)} %broadcast_in_dim.33), channel_id=1, replica_groups={{0,64,128,192,256,320,384,448},{16,80,144,208,272,336,400,464},{32,96,1..., dimensions={0} | all-to-all | bytes 819200 | tf_op jit(solution)/shard_map/all_to_all | solution.py:116
  44.6 0.1 slice_bitcast_fusion
  44.7 0.0 copy-start
  44.7 0.0 copy-start.1
  44.7 2.2 %collective-permute-start = (bf16[4,192,128]{2,1,0:T(8,128)(2,1)S(1)}, bf16[4,192,128]{2,1,0:T(8,128)(2,1)S(1)}, u32[]{:S(2)}, u32[]{:S(2)}) collective-permute-start(bf16[4,192,128]{2,1,0:T(8,128)(2,1)S(1)} %get-tuple-element.14.refs_0_), channel_id=1, source_target_pairs={{0,16},{16,0},{32,48},{48,32},{64,80},{80,64},{96,112},{112,96},{1... | collective-permute-start | bytes 589832 | tf_op jit(solution)/shard_map/ppermute | solution.py:26
  46.9 2.5 %collective-permute-start.2 = (bf16[4,192,128]{2,1,0:T(8,128)(2,1)S(1)}, bf16[4,192,128]{2,1,0:T(8,128)(2,1)S(1)}, u32[]{:S(2)}, u32[]{:S(2)}) collective-permute-start(bf16[4,192,128]{2,1,0:T(8,128)(2,1)S(1)} %get-tuple-element.13.refs_3_), channel_id=1, source_target_pairs={{0,48},{16,32},{32,16},{48,0},{64,112},{80,96},{96,80},{112,64},{1... | collective-permute-start | bytes 589832 | tf_op jit(solution)/shard_map/ppermute | solution.py:26
  49.4 2.1 %collective-permute-done.refs_1_ = bf16[4,192,128]{2,1,0:T(8,128)(2,1)S(1)} collective-permute-done((bf16[4,192,128]{2,1,0:T(8,128)(2,1)S(1)}, bf16[4,192,128]{2,1,0:T(8,128)(2,1)S(1)}, u32[]{:S(2)}, u32[]{:S(2)}) %collective-permute-start) | collective-permute-done | bytes 196640 | tf_op jit(solution)/shard_map/ppermute | solution.py:26
  51.5 0.0 copy-start.2
  51.6 2.8 %collective-permute-start.1 = (bf16[2,4,192,128]{3,2,1,0:T(8,128)(2,1)S(1)}, bf16[2,4,192,128]{3,2,1,0:T(8,128)(2,1)S(1)}, u32[]{:S(2)}, u32[]{:S(2)}) collective-permute-start(bf16[2,4,192,128]{3,2,1,0:T(8,128)(2,1)S(1)} %pad_maximum_fusion), channel_id=1, source_target_pairs={{0,48},{16,32},{32,16},{48,0},{64,112},{80,96},{96,80},{112,64},{1... | collective-permute-start | bytes 1179656 | tf_op jit(solution)/shard_map/ppermute | solution.py:26
  54.4 0.6 collective-permute-done.2.refs_4_
  54.9 0.0 copy-start.3
  55.0 1.9 %collective-permute-start.3 = (bf16[2,4,192,128]{3,2,1,0:T(8,128)(2,1)S(1)}, bf16[2,4,192,128]{3,2,1,0:T(8,128)(2,1)S(1)}, u32[]{:S(2)}, u32[]{:S(2)}) collective-permute-start(bf16[2,4,192,128]{3,2,1,0:T(8,128)(2,1)S(1)} %pad_maximum_fusion.1), channel_id=1, source_target_pairs={{0,16},{16,0},{32,48},{48,32},{64,80},{80,64},{96,112},{112,96},{1... | collective-permute-start | bytes 1179656 | tf_op jit(solution)/shard_map/ppermute | solution.py:26
  57.0 28.4 %all_to_all.17 = bf16[16,24,128]{2,1,0:T(8,128)(2,1)S(1)} all-to-all(bf16[16,24,128]{2,1,0:T(8,128)(2,1)S(1)} %broadcast_in_dim.39), channel_id=1, replica_groups=mesh['zero'=32,'width'=16] {'width'}, dimensions={0} | all-to-all | bytes 196608 | tf_op jit(solution)/shard_map/all_to_all | solution.py:120
  85.3 0.6 reduce_sum.25
  85.9 0.0 collective-permute-done.1.refs_2_
  86.0 0.0 collective-permute-done.3.refs_5_
  86.0 0.0 copy-done
  86.0 0.0 copy-done.1
  86.0 0.0 copy-done.2
  86.0 0.0 copy-done.3
  86.0 0.7 copy-done.4
  86.7 0.8 copy-done.5
  87.5 2.8 %last.1.up_in = bf16[512,3072]{1,0:T(8,128)(2,1)} custom-call(bf16[4,192,128]{2,1,0:T(8,128)(2,1)} %copy-done.1, bf16[4,192,128]{2,1,0:T(8,128)(2,1)} %copy-done.2, bf16[2,4,192,128]{3,2,1,0:T(8,128)(2,1)} %copy-done.4, bf16[4,192,128]{2,1,0:T(8,128)(2,1)} %copy-done, bf16[4,192,128]{2,1,0:T(8,128)(2,1)} %copy-done.3, bf16[2,4,192,128]{3,2,1,0:T(8,128)(2,1)} %copy-done.5), custom_call_target="tpu_custom_call" | custom-call | tf_op jit(solution)/shard_map/last/pallas_call | solution.py:142
  90.2 0.7 all-gather.3.cloned.1.call-done
  90.9 3.9 %first.1 = (bf16[512,3072]{1,0:T(8,128)(2,1)}, bf16[512,3072]{1,0:T(8,128)(2,1)}) custom-call(bf16[8,4,584,128]{3,2,1,0:T(8,128)(2,1)} %bitcast.12, bf16[512,3072]{1,0:T(8,128)(2,1)} %last.1.up_in), custom_call_target="tpu_custom_call", output_to_operand_aliasing={{1}: (1, {})} | custom-call | tf_op jit(solution)/shard_map/first/pallas_call | solution.py:146
  (7 shorter events, 0.1 us)
Async XLA Ops:
  7.2 83.8 %all-gather.3.cloned.1.call-start = ((), (), s32[]{:S(2)}) async-start(), calls=%async_computation.3 | async-start | bytes 5382144 | tf_op jit(solution)/shard_map/all_gather | solution.py:112
  44.7 41.3 %copy-start = (bf16[4,192,128]{2,1,0:T(8,128)(2,1)}, bf16[4,192,128]{2,1,0:T(8,128)(2,1)S(1)}, u32[]{:S(2)}) copy-start(bf16[4,192,128]{2,1,0:T(8,128)(2,1)S(1)} %get-tuple-element.13.refs_3_) | copy-start | bytes 589828
  44.7 41.3 %copy-start.1 = (bf16[4,192,128]{2,1,0:T(8,128)(2,1)}, bf16[4,192,128]{2,1,0:T(8,128)(2,1)S(1)}, u32[]{:S(2)}) copy-start(bf16[4,192,128]{2,1,0:T(8,128)(2,1)S(1)} %get-tuple-element.14.refs_0_) | copy-start | bytes 589828
  44.7 6.8 %collective-permute-start = (bf16[4,192,128]{2,1,0:T(8,128)(2,1)S(1)}, bf16[4,192,128]{2,1,0:T(8,128)(2,1)S(1)}, u32[]{:S(2)}, u32[]{:S(2)}) collective-permute-start(bf16[4,192,128]{2,1,0:T(8,128)(2,1)S(1)} %get-tuple-element.14.refs_0_), channel_id=1, source_target_pairs={{0,16},{16,0},{32,48},{48,32},{64,80},{80,64},{96,112},{112,96},{1... | collective-permute-start | bytes 589832 | tf_op jit(solution)/shard_map/ppermute | solution.py:26
  46.9 8.0 %collective-permute-start.2 = (bf16[4,192,128]{2,1,0:T(8,128)(2,1)S(1)}, bf16[4,192,128]{2,1,0:T(8,128)(2,1)S(1)}, u32[]{:S(2)}, u32[]{:S(2)}) collective-permute-start(bf16[4,192,128]{2,1,0:T(8,128)(2,1)S(1)} %get-tuple-element.13.refs_3_), channel_id=1, source_target_pairs={{0,48},{16,32},{32,16},{48,0},{64,112},{80,96},{96,80},{112,64},{1... | collective-permute-start | bytes 589832 | tf_op jit(solution)/shard_map/ppermute | solution.py:26
  51.5 34.4 %copy-start.2 = (bf16[4,192,128]{2,1,0:T(8,128)(2,1)}, bf16[4,192,128]{2,1,0:T(8,128)(2,1)S(1)}, u32[]{:S(2)}) copy-start(bf16[4,192,128]{2,1,0:T(8,128)(2,1)S(1)} %collective-permute-done.refs_1_) | copy-start | bytes 589828
  51.6 34.4 %collective-permute-start.1 = (bf16[2,4,192,128]{3,2,1,0:T(8,128)(2,1)S(1)}, bf16[2,4,192,128]{3,2,1,0:T(8,128)(2,1)S(1)}, u32[]{:S(2)}, u32[]{:S(2)}) collective-permute-start(bf16[2,4,192,128]{3,2,1,0:T(8,128)(2,1)S(1)} %pad_maximum_fusion), channel_id=1, source_target_pairs={{0,48},{16,32},{32,16},{48,0},{64,112},{80,96},{96,80},{112,64},{1... | collective-permute-start | bytes 1179656 | tf_op jit(solution)/shard_map/ppermute | solution.py:26
  54.9 31.0 %copy-start.3 = (bf16[4,192,128]{2,1,0:T(8,128)(2,1)}, bf16[4,192,128]{2,1,0:T(8,128)(2,1)S(1)}, u32[]{:S(2)}) copy-start(bf16[4,192,128]{2,1,0:T(8,128)(2,1)S(1)} %collective-permute-done.2.refs_4_) | copy-start | bytes 589828
  55.0 31.0 %collective-permute-start.3 = (bf16[2,4,192,128]{3,2,1,0:T(8,128)(2,1)S(1)}, bf16[2,4,192,128]{3,2,1,0:T(8,128)(2,1)S(1)}, u32[]{:S(2)}, u32[]{:S(2)}) collective-permute-start(bf16[2,4,192,128]{3,2,1,0:T(8,128)(2,1)S(1)} %pad_maximum_fusion.1), channel_id=1, source_target_pairs={{0,16},{16,0},{32,48},{48,32},{64,80},{80,64},{96,112},{112,96},{1... | collective-permute-start | bytes 1179656 | tf_op jit(solution)/shard_map/ppermute | solution.py:26
  85.9 0.7 copy-start.4
  86.7 0.8 copy-start.5
Sparse Core Ops, SparseCore 0:
  21.7 69.2 all-gather.2

commit v4 on v3

--- a/solution.py
+++ b/solution.py
@@ -9,7 +9,7 @@
 mix_rate = 1.0
 LANES, PIECE = 128, 96
 NY, NX, NW = 8, 4, 16
-N_FIRST = 6
+N_FIRST = 5
 N_LAST = 8 - N_FIRST
 ROWS_FIRST = N_FIRST * PIECE + 8
 ROWS_LAST = N_LAST * PIECE
@@ -67,13 +67,11 @@
                 stage.at[y, pl.ds(at, rows), :], out.at[pl.ds(row, rows), pl.ds(y * 384, 384)], sem_out.at[k, y])
             cp.start()
             stores.append(cp)
-    for cp in stores:
-        cp.wait()
+    return stores
 
 
-def last_kernel(*refs):
+def fetch_last(ins, buf, sem_in):
     x = lax.axis_index("zero") & (NX - 1)
-    ins, (up, buf, stage, sem_in, sem_out) = refs[:6], refs[6:]
     fetch = []
     for y in range(NY):
         h, g = divmod(y, NY // 2)
@@ -86,16 +84,20 @@
         ])
         for cp in fetch[-1]:
             cp.start()
-    n = N_LAST * LANES
-    assemble(fetch, N_LAST, [(up, 0, 512 - n, n)], buf, stage, sem_out)
+    return fetch
 
 
-def first_kernel(got, up_in, gate, up, buf, stage, sem_in, sem_out):
+def place_kernel(got, *refs):
+    parts, (gate, up, buf, stage, sem_in, sem_out, buf_l, stage_l, sem_in_l, sem_out_l) = refs[:6], refs[6:]
     fetch = [[pltpu.make_async_copy(got.at[y], buf.at[y], sem_in.at[y])] for y in range(NY)]
     for cps in fetch:
         cps[0].start()
-    n = (N_FIRST - 4) * LANES
-    assemble(fetch, N_FIRST, [(gate, 0, 0, 512), (up, 512, 0, n)], buf, stage, sem_out)
+    late = fetch_last(parts, buf_l, sem_in_l)
+    n, m = (N_FIRST - 4) * LANES, N_LAST * LANES
+    stores = assemble(fetch, N_FIRST, [(gate, 0, 0, 512), (up, 512, 0, n)], buf, stage, sem_out)
+    stores += assemble(late, N_LAST, [(up, 0, 512 - m, m)], buf_l, stage_l, sem_out_l)
+    for cp in stores:
+        cp.wait()
 
 
 def program(w_gate, low_gate, high_gate, w_up, low_up, high_up, norm_train, norm_step):
@@ -117,13 +119,18 @@
         jnp.broadcast_to(own[None], (NY,) + own.shape), "zero", 0, 0, tiled=True, axis_index_groups=Y_ROWS)
 
     norm_xy = along_y[:, ROWS_LAST:ROWS_LAST + 3].reshape(24, LANES)
-    spread = lax.all_to_all(jnp.broadcast_to(norm_xy[None], (NW, 24, LANES)), "width", 0, 0, tiled=True)
+    norm_xy = norm_xy + lax.ppermute(norm_xy, "width", [(w, w ^ 1) for w in range(NW)])
+    spread = lax.all_to_all(
+        jnp.broadcast_to(norm_xy[None], (NW // 2, 24, LANES)), "width", 0, 0, tiled=True,
+        axis_index_groups=[[2 * z + core for z in range(NW // 2)] for core in range(2)])
     serve_norm = jnp.sum(spread.astype(jnp.float32), axis=0).astype(bf16).reshape(3072)
 
     halves = []
     for h in range(2):
         a = along_y[h * 4:(h + 1) * 4, :ROWS_LAST]
         halves.append((a, swap(a, h)))
+    near = lax.optimization_barrier(tuple(b for _, b in halves))
+    halves = [(a, b) for (a, _), b in zip(halves, near)]
     both = [jnp.concatenate([a[None], b[None]], axis=0) for a, b in halves]
     parts = []
     for h in range(2):
@@ -139,14 +146,10 @@
             pltpu.SemaphoreType.DMA((n_out, NY)),
         ]
 
-    up = pl.pallas_call(
-        last_kernel, in_specs=[hb] * 6, out_specs=hb, out_shape=out,
-        scratch_shapes=scratch(ROWS_LAST, N_LAST, 1, (NY, NX)), name="last",
-    )(*parts)
     gate, up = pl.pallas_call(
-        first_kernel, in_specs=[hb, hb], out_specs=[hb, hb], out_shape=[out, out],
-        scratch_shapes=scratch(ROWS_FIRST, N_FIRST, 2, (NY,)), input_output_aliases={1: 1}, name="first",
-    )(got_first, up)
+        place_kernel, in_specs=[hb] * 7, out_specs=[hb, hb], out_shape=[out, out],
+        scratch_shapes=scratch(ROWS_FIRST, N_FIRST, 2, (NY,)) + scratch(ROWS_LAST, N_LAST, 1, (NY, NX)), name="place",
+    )(got_first, *parts)
     return (gate, up, serve_norm)
 
 

time: 102 us -> 111 us (1.088)
  starting transfers between devices: 9.42 us -> 19.9 us
  blocking collectives: 62.1 us -> 57 us
  waiting for transfers between devices: 3.41 us -> 6.78 us
    ppermute x0 -> x1, starting transfers between devices: none -> 9.52 us  [program(): lax.ppermute(norm_xy, 'width', [(w, w ^ 1) for w in range(NW)])]
    all_to_all x1, blocking collectives: 28.4 us -> 19.7 us  [program(): lax.all_to_all(jnp.broadcast_to(norm_xy[None], (NW // 2, 24, LANES)), 'wi...]
    all_to_all x1, blocking collectives: 21.5 us -> 25.5 us  [program(): lax.all_to_all(jnp.broadcast_to(own[None], (NY,) + own.shape), 'zero', 0,...]
    ppermute x4, waiting for transfers between devices: 2.7 us -> 5.94 us  [swap(): return lax.ppermute(a, 'zero', pairs)]
    pallas_call x2 -> x1, Pallas kernels: 6.71 us -> 5.76 us  [program(): pl.pallas_call(place_kernel, in_specs=[hb] * 7, out_specs=[hb, hb], out_s...]
  transfers between devices with their start and end apart: 5 -> 6, of which waited for: 3 -> 3; matrix products, arithmetic and copies ran while one was open for 2% -> 3% of each run, Pallas kernels for 3% -> 0%
where the time goes in v4:
time: 111 us; the launch traced here: 110 us
  blocking collectives  57 us (51%)
  starting transfers between devices  19.9 us (18%)
  between operations  14.2 us (13%)
  Pallas kernels  7.78 us (7%)
  waiting for transfers between devices  6.78 us (6%)
  other arithmetic  3.14 us (3%)
  local copies, waits for them, and re-layouts  1.21 us (1%)
    all_to_all x1, blocking collectives, program(): lax.all_to_all(jnp.broadcast_to(own[None], (NY,) + own.shape), 'zero', 0,...  25.5 us
    all_to_all x1, blocking collectives, program(): lax.all_to_all(jnp.broadcast_to(norm_xy[None], (NW // 2, 24, LANES)), 'wi...  19.7 us
    all_to_all x1, blocking collectives, program(): lax.all_to_all(first, 'zero', 0, 0, tiled=True, axis_index_groups=X_ROWS)  11.7 us
    ppermute x4, starting transfers between devices, swap(): return lax.ppermute(a, 'zero', pairs)  10.3 us
    ppermute x1, starting transfers between devices, program(): lax.ppermute(norm_xy, 'width', [(w, w ^ 1) for w in range(NW)])  9.52 us
    ppermute x4, waiting for transfers between devices, swap(): return lax.ppermute(a, 'zero', pairs)  5.94 us
    pallas_call x1, Pallas kernels, program(): pl.pallas_call(place_kernel, in_specs=[hb] * 7, out_specs=[hb, hb], out_s...  5.76 us
  transfers between devices with their start and end apart: 6, of which 3 were waited for; matrix products, arithmetic and copies ran while one was open for 3% of the time, Pallas kernels for 0%

profile of v4, /device:TPU:1, one launch (start us, length us, event | category | flops | bytes accessed | tf_op | source)
XLA Modules:
  0.0 110.0 jit_solution(6099669544377579424)
XLA Ops:
  7.2 0.0 all-gather.3.cloned.1.call-start
  7.2 2.0 %merge.1 = (bf16[4,488,128]{2,1,0:T(8,128)(2,1)}, bf16[288,128]{1,0:T(8,128)(2,1)}) custom-call(bf16[96,512]{1,0:T(8,128)(2,1)} %wg.1, bf16[16,96]{1,0:T(8,128)(2,1)} %bitcast.16, bf16[16,512]{1,0:T(8,128)(2,1)} %hg.1, bf16[96,512]{1,0:T(8,128)(2,1)} %wu.1, bf16[16,96]{1,0:T(8,128)(2,1)} %bitcast.17, bf16[16,512]{1,0:T(8,128)(2,1)} %hu.1, f32[1,6]{1,0:T(1,128)} %bitcast.18, ...), custom_call_target="tpu_custom_call" | custom-call | tf_op jit(solution)/shard_map/merge/pallas_call | solution.py:107
  9.2 11.7 %all_to_all.15 = bf16[4,488,128]{2,1,0:T(8,128)(2,1)} all-to-all(bf16[4,488,128]{2,1,0:T(8,128)(2,1)} %get-tuple-element.9), channel_id=1, replica_groups={{0,16,32,48},{64,80,96,112},{128,144,160,176},{192,208,224,240},{256,27..., dimensions={0} | all-to-all | bytes 999424 | tf_op jit(solution)/shard_map/all_to_all | solution.py:113
  21.0 0.0 all-gather.3.cloned.1.call-update
  21.0 0.7 slice_reduce_fusion
  21.7 0.9 pad_maximum_fusion.2
  22.6 0.1 broadcast_in_dim.32
  22.7 25.5 %all_to_all.16 = bf16[8,296,128]{2,1,0:T(8,128)(2,1)S(1)} all-to-all(bf16[8,296,128]{2,1,0:T(8,128)(2,1)S(1)} %broadcast_in_dim.32), channel_id=1, replica_groups={{0,64,128,192,256,320,384,448},{16,80,144,208,272,336,400,464},{32,96,1..., dimensions={0} | all-to-all | bytes 1212416 | tf_op jit(solution)/shard_map/all_to_all | solution.py:118
  48.2 0.2 slice_bitcast_fusion
  48.3 0.0 copy-start
  48.4 2.1 %collective-permute-start.1 = (bf16[4,288,128]{2,1,0:T(8,128)(2,1)S(1)}, bf16[4,288,128]{2,1,0:T(8,128)(2,1)S(1)}, u32[]{:S(2)}, u32[]{:S(2)}) collective-permute-start(bf16[4,288,128]{2,1,0:T(8,128)(2,1)S(1)} %get-tuple-element.17.refs_3_), channel_id=1, source_target_pairs={{0,48},{16,32},{32,16},{48,0},{64,112},{80,96},{96,80},{112,64},{1... | collective-permute-start | bytes 884744 | tf_op jit(solution)/shard_map/ppermute | solution.py:26
  50.5 1.9 %collective-permute-start = (bf16[4,288,128]{2,1,0:T(8,128)(2,1)S(1)}, bf16[4,288,128]{2,1,0:T(8,128)(2,1)S(1)}, u32[]{:S(2)}, u32[]{:S(2)}) collective-permute-start(bf16[4,288,128]{2,1,0:T(8,128)(2,1)S(1)} %get-tuple-element.18.refs_0_), channel_id=1, source_target_pairs={{0,16},{16,0},{32,48},{48,32},{64,80},{80,64},{96,112},{112,96},{1... | collective-permute-start | bytes 884744 | tf_op jit(solution)/shard_map/ppermute | solution.py:26
  52.4 5.0 %collective-permute-done.1.refs_4_ = bf16[4,288,128]{2,1,0:T(8,128)(2,1)S(1)} collective-permute-done((bf16[4,288,128]{2,1,0:T(8,128)(2,1)S(1)}, bf16[4,288,128]{2,1,0:T(8,128)(2,1)S(1)}, u32[]{:S(2)}, u32[]{:S(2)}) %collective-permute-start.1) | collective-permute-done | bytes 294944 | tf_op jit(solution)/shard_map/ppermute | solution.py:26
  57.4 0.9 collective-permute-done.refs_1_
  58.4 0.1 pad_maximum_fusion
  58.4 4.4 %collective-permute-start.2 = (bf16[2,4,288,128]{3,2,1,0:T(8,128)(2,1)S(1)}, bf16[2,4,288,128]{3,2,1,0:T(8,128)(2,1)S(1)}, u32[]{:S(2)}, u32[]{:S(2)}) collective-permute-start(bf16[2,4,288,128]{3,2,1,0:T(8,128)(2,1)S(1)} %pad_maximum_fusion), channel_id=1, source_target_pairs={{0,48},{16,32},{32,16},{48,0},{64,112},{80,96},{96,80},{112,64},{1... | collective-permute-start | bytes 1769480 | tf_op jit(solution)/shard_map/ppermute | solution.py:26
  62.8 0.1 pad_maximum_fusion.1
  62.9 1.9 %collective-permute-start.3 = (bf16[2,4,288,128]{3,2,1,0:T(8,128)(2,1)S(1)}, bf16[2,4,288,128]{3,2,1,0:T(8,128)(2,1)S(1)}, u32[]{:S(2)}, u32[]{:S(2)}) collective-permute-start(bf16[2,4,288,128]{3,2,1,0:T(8,128)(2,1)S(1)} %pad_maximum_fusion.1), channel_id=1, source_target_pairs={{0,16},{16,0},{32,48},{48,32},{64,80},{80,64},{96,112},{112,96},{1... | collective-permute-start | bytes 1769480 | tf_op jit(solution)/shard_map/ppermute | solution.py:26
  64.8 9.5 %collective-permute-start.4 = (bf16[24,128]{1,0:T(8,128)(2,1)S(1)}, bf16[24,128]{1,0:T(8,128)(2,1)S(1)}, u32[]{:S(2)}, u32[]{:S(2)}) collective-permute-start(bf16[24,128]{1,0:T(8,128)(2,1)S(1)} %reshape.14), channel_id=1, source_target_pairs={{0,1},{1,0},{2,3},{3,2},{4,5},{5,4},{6,7},{7,6},{8,9},{9,8},{10,11... | collective-permute-start | bytes 18440 | tf_op jit(solution)/shard_map/ppermute | solution.py:122
  74.4 0.8 collective-permute-done.4
  75.2 19.7 %all_to_all.17 = bf16[8,24,128]{2,1,0:T(8,128)(2,1)} all-to-all(bf16[8,24,128]{2,1,0:T(8,128)(2,1)S(1)} %broadcast_in_dim.37), channel_id=1, replica_groups={{0,2,4,6,8,10,12,14},{1,3,5,7,9,11,13,15},{16,18,20,22,24,26,28,30},{17..., dimensions={0} | all-to-all | bytes 98304 | tf_op jit(solution)/shard_map/all_to_all | solution.py:123
  94.9 1.4 %reduce_sum.25 = bf16[24,128]{1,0:T(8,128)(2,1)} reduce(bf16[8,24,128]{2,1,0:T(8,128)(2,1)} %all_to_all.17, bf16[]{:T(256)} %constant.3.clone.1), dimensions={0}, to_apply=%region_1.0 | reduce | flops 21504 | bytes 55298 | tf_op jit(solution)/shard_map/reduce_sum | solution.py:126
  96.3 0.0 collective-permute-done.2.refs_2_
  96.3 0.0 collective-permute-done.3.refs_5_
  96.3 0.0 all-gather.3.cloned.1.call-done
  96.4 0.0 copy-done
  96.4 0.0 copy-done.1
  96.4 0.0 copy-done.2
  96.4 0.0 copy-done.3
  96.4 0.7 copy-done.4
  97.2 0.2 copy-done.5
  97.3 5.8 %place.1 = (bf16[512,3072]{1,0:T(8,128)(2,1)}, bf16[512,3072]{1,0:T(8,128)(2,1)}) custom-call(bf16[8,4,488,128]{3,2,1,0:T(8,128)(2,1)} %bitcast.12, bf16[4,288,128]{2,1,0:T(8,128)(2,1)} %copy-done.1, bf16[4,288,128]{2,1,0:T(8,128)(2,1)} %copy-done.3, bf16[2,4,288,128]{3,2,1,0:T(8,128)(2,1)} %copy-done.4, bf16[4,288,128]{2,1,0:T(8,128)(2,1)} %copy-done, ...), custom_call_target="tpu_custom_call" | custom-call | tf_op jit(solution)/shard_map/place/pallas_call | solution.py:149
  (9 shorter events, 0.1 us)
Async XLA Ops:
  7.2 89.2 %all-gather.3.cloned.1.call-start = ((), (), s32[]{:S(2)}) async-start(), calls=%async_computation.3 | async-start | bytes 4497408 | tf_op jit(solution)/shard_map/all_gather | solution.py:114
  48.3 48.0 %copy-start = (bf16[4,288,128]{2,1,0:T(8,128)(2,1)}, bf16[4,288,128]{2,1,0:T(8,128)(2,1)S(1)}, u32[]{:S(2)}) copy-start(bf16[4,288,128]{2,1,0:T(8,128)(2,1)S(1)} %get-tuple-element.17.refs_3_) | copy-start | bytes 884740
  48.4 48.0 %copy-start.1 = (bf16[4,288,128]{2,1,0:T(8,128)(2,1)}, bf16[4,288,128]{2,1,0:T(8,128)(2,1)S(1)}, u32[]{:S(2)}) copy-start(bf16[4,288,128]{2,1,0:T(8,128)(2,1)S(1)} %get-tuple-element.18.refs_0_) | copy-start | bytes 884740
  48.4 9.1 %collective-permute-start.1 = (bf16[4,288,128]{2,1,0:T(8,128)(2,1)S(1)}, bf16[4,288,128]{2,1,0:T(8,128)(2,1)S(1)}, u32[]{:S(2)}, u32[]{:S(2)}) collective-permute-start(bf16[4,288,128]{2,1,0:T(8,128)(2,1)S(1)} %get-tuple-element.17.refs_3_), channel_id=1, source_target_pairs={{0,48},{16,32},{32,16},{48,0},{64,112},{80,96},{96,80},{112,64},{1... | collective-permute-start | bytes 884744 | tf_op jit(solution)/shard_map/ppermute | solution.py:26
  50.5 7.9 %collective-permute-start = (bf16[4,288,128]{2,1,0:T(8,128)(2,1)S(1)}, bf16[4,288,128]{2,1,0:T(8,128)(2,1)S(1)}, u32[]{:S(2)}, u32[]{:S(2)}) collective-permute-start(bf16[4,288,128]{2,1,0:T(8,128)(2,1)S(1)} %get-tuple-element.18.refs_0_), channel_id=1, source_target_pairs={{0,16},{16,0},{32,48},{48,32},{64,80},{80,64},{96,112},{112,96},{1... | collective-permute-start | bytes 884744 | tf_op jit(solution)/shard_map/ppermute | solution.py:26
  57.4 39.0 %copy-start.2 = (bf16[4,288,128]{2,1,0:T(8,128)(2,1)}, bf16[4,288,128]{2,1,0:T(8,128)(2,1)S(1)}, u32[]{:S(2)}) copy-start(bf16[4,288,128]{2,1,0:T(8,128)(2,1)S(1)} %collective-permute-done.1.refs_4_) | copy-start | bytes 884740
  58.4 38.0 %copy-start.3 = (bf16[4,288,128]{2,1,0:T(8,128)(2,1)}, bf16[4,288,128]{2,1,0:T(8,128)(2,1)S(1)}, u32[]{:S(2)}) copy-start(bf16[4,288,128]{2,1,0:T(8,128)(2,1)S(1)} %collective-permute-done.refs_1_) | copy-start | bytes 884740
  58.4 37.9 %collective-permute-start.2 = (bf16[2,4,288,128]{3,2,1,0:T(8,128)(2,1)S(1)}, bf16[2,4,288,128]{3,2,1,0:T(8,128)(2,1)S(1)}, u32[]{:S(2)}, u32[]{:S(2)}) collective-permute-start(bf16[2,4,288,128]{3,2,1,0:T(8,128)(2,1)S(1)} %pad_maximum_fusion), channel_id=1, source_target_pairs={{0,48},{16,32},{32,16},{48,0},{64,112},{80,96},{96,80},{112,64},{1... | collective-permute-start | bytes 1769480 | tf_op jit(solution)/shard_map/ppermute | solution.py:26
  62.9 33.5 %collective-permute-start.3 = (bf16[2,4,288,128]{3,2,1,0:T(8,128)(2,1)S(1)}, bf16[2,4,288,128]{3,2,1,0:T(8,128)(2,1)S(1)}, u32[]{:S(2)}, u32[]{:S(2)}) collective-permute-start(bf16[2,4,288,128]{3,2,1,0:T(8,128)(2,1)S(1)} %pad_maximum_fusion.1), channel_id=1, source_target_pairs={{0,16},{16,0},{32,48},{48,32},{64,80},{80,64},{96,112},{112,96},{1... | collective-permute-start | bytes 1769480 | tf_op jit(solution)/shard_map/ppermute | solution.py:26
  64.8 10.3 %collective-permute-start.4 = (bf16[24,128]{1,0:T(8,128)(2,1)S(1)}, bf16[24,128]{1,0:T(8,128)(2,1)S(1)}, u32[]{:S(2)}, u32[]{:S(2)}) collective-permute-start(bf16[24,128]{1,0:T(8,128)(2,1)S(1)} %reshape.14), channel_id=1, source_target_pairs={{0,1},{1,0},{2,3},{3,2},{4,5},{5,4},{6,7},{7,6},{8,9},{9,8},{10,11... | collective-permute-start | bytes 18440 | tf_op jit(solution)/shard_map/ppermute | solution.py:122
  96.3 0.8 copy-start.4
  96.3 1.0 copy-start.5
Sparse Core Ops, SparseCore 0:
  21.1 64.9 all-gather.2

commit v5 on v4

--- a/solution.py
+++ b/solution.py
@@ -49,9 +49,12 @@
             for x in range(NX):
                 first[x, t * PIECE:(t + 1) * PIECE, :] = tile
         else:
-            last[(t - N_FIRST) * PIECE:(t - N_FIRST + 1) * PIECE, :] = tile
+            for y in range(NY):
+                last[y, (t - N_FIRST) * PIECE:(t - N_FIRST + 1) * PIECE, :] = tile
     for x in range(NX):
         first[x, N_FIRST * PIECE:, :] = rows
+    for y in range(NY):
+        last[y, ROWS_LAST:, :] = jnp.zeros((8, LANES), jnp.bfloat16)
 
 
 def assemble(fetch, tiles, outs, buf, stage, sem_out):
@@ -106,7 +109,7 @@
     bf16 = jnp.bfloat16
     first, last = pl.pallas_call(
         merge_kernel, in_specs=[vm] * 8, out_specs=[vm, vm],
-        out_shape=[jax.ShapeDtypeStruct((NX, ROWS_FIRST, LANES), bf16), jax.ShapeDtypeStruct((ROWS_LAST, LANES), bf16)],
+        out_shape=[jax.ShapeDtypeStruct((NX, ROWS_FIRST, LANES), bf16), jax.ShapeDtypeStruct((NY, ROWS_LAST + 8, LANES), bf16)],
         name="merge",
     )(w_gate, low_gate.T, high_gate, w_up, low_up.T, high_up, norm_train[None, :], norm_step[None, :])
 
@@ -114,9 +117,8 @@
     got_first = lax.all_gather(along_x, "zero", axis=0, axis_index_groups=Y_ROWS)
 
     norm_x = jnp.sum(along_x[:, N_FIRST * PIECE:, :].astype(jnp.float32), axis=0).astype(bf16)
-    own = jnp.concatenate([last, norm_x], axis=0)
-    along_y = lax.all_to_all(
-        jnp.broadcast_to(own[None], (NY,) + own.shape), "zero", 0, 0, tiled=True, axis_index_groups=Y_ROWS)
+    own = lax.dynamic_update_slice(last, jnp.broadcast_to(norm_x[None], (NY, 8, LANES)), (0, ROWS_LAST, 0))
+    along_y = lax.all_to_all(own, "zero", 0, 0, tiled=True, axis_index_groups=Y_ROWS)
 
     norm_xy = along_y[:, ROWS_LAST:ROWS_LAST + 3].reshape(24, LANES)
     norm_xy = norm_xy + lax.ppermute(norm_xy, "width", [(w, w ^ 1) for w in range(NW)])

time: 111 us -> 112 us (level)
    concatenate x2, other arithmetic: 0.11 us -> 1.78 us  [program(): both = [jnp.concatenate([a[None], b[None]], axis=0) for a, b in halves]]
  transfers between devices with their start and end apart: 6 -> 6, of which waited for: 3 -> 3; matrix products, arithmetic and copies ran while one was open for 3% -> 4% of each run, Pallas kernels for 0% -> 0%
where the time goes in v5:
time: 112 us; the launch traced here: 111 us
  blocking collectives  57 us (51%)
  starting transfers between devices  19.8 us (18%)
  between operations  14.2 us (13%)
  Pallas kernels  7.98 us (7%)
  waiting for transfers between devices  6.78 us (6%)
  other arithmetic  3.11 us (3%)
  local copies, waits for them, and re-layouts  1.74 us (2%)
    all_to_all x1, blocking collectives, program(): lax.all_to_all(own, 'zero', 0, 0, tiled=True, axis_index_groups=Y_ROWS)  25.5 us
    all_to_all x1, blocking collectives, program(): lax.all_to_all(jnp.broadcast_to(norm_xy[None], (NW // 2, 24, LANES)), 'wi...  19.8 us
    all_to_all x1, blocking collectives, program(): lax.all_to_all(first, 'zero', 0, 0, tiled=True, axis_index_groups=X_ROWS)  11.7 us
    ppermute x4, starting transfers between devices, swap(): return lax.ppermute(a, 'zero', pairs)  10.3 us
    ppermute x1, starting transfers between devices, program(): lax.ppermute(norm_xy, 'width', [(w, w ^ 1) for w in range(NW)])  9.5 us
    ppermute x4, waiting for transfers between devices, swap(): return lax.ppermute(a, 'zero', pairs)  5.94 us
    pallas_call x1, Pallas kernels, program(): pl.pallas_call(place_kernel, in_specs=[hb] * 7, out_specs=[hb, hb], out_s...  5.76 us
  transfers between devices with their start and end apart: 6, of which 3 were waited for; matrix products, arithmetic and copies ran while one was open for 4% of the time, Pallas kernels for 0%

profile of v5, /device:TPU:1, one launch (start us, length us, event | category | flops | bytes accessed | tf_op | source)
XLA Modules:
  0.0 110.7 jit_solution(4208410731211115677)
XLA Ops:
  7.2 0.0 all-gather.3.cloned.1.call-start
  7.2 2.2 %merge.1 = (bf16[4,488,128]{2,1,0:T(8,128)(2,1)}, bf16[8,296,128]{2,1,0:T(8,128)(2,1)}) custom-call(bf16[96,512]{1,0:T(8,128)(2,1)} %wg.1, bf16[16,96]{1,0:T(8,128)(2,1)} %bitcast.16, bf16[16,512]{1,0:T(8,128)(2,1)} %hg.1, bf16[96,512]{1,0:T(8,128)(2,1)} %wu.1, bf16[16,96]{1,0:T(8,128)(2,1)} %bitcast.17, bf16[16,512]{1,0:T(8,128)(2,1)} %hu.1, ...), custom_call_target="tpu_custom_call" | custom-call | tf_op jit(solution)/shard_map/merge/pallas_call | solution.py:110
  9.4 11.7 %all_to_all.15 = bf16[4,488,128]{2,1,0:T(8,128)(2,1)} all-to-all(bf16[4,488,128]{2,1,0:T(8,128)(2,1)} %get-tuple-element.9), channel_id=1, replica_groups={{0,16,32,48},{64,80,96,112},{128,144,160,176},{192,208,224,240},{256,27..., dimensions={0} | all-to-all | bytes 999424 | tf_op jit(solution)/shard_map/all_to_all | solution.py:116
  21.2 0.0 all-gather.3.cloned.1.call-update
  21.2 0.7 slice_reduce_fusion
  21.9 0.6 broadcast_dynamic-update-slice_fusion
  22.5 25.5 %all_to_all.16 = bf16[8,296,128]{2,1,0:T(8,128)(2,1)S(1)} all-to-all(bf16[8,296,128]{2,1,0:T(8,128)(2,1)} %broadcast_dynamic-update-slice_fusion), channel_id=1, replica_groups={{0,64,128,192,256,320,384,448},{16,80,144,208,272,336,400,464},{32,96,1..., dimensions={0} | all-to-all | bytes 1212416 | tf_op jit(solution)/shard_map/all_to_all | solution.py:121
  48.1 0.2 slice_bitcast_fusion
  48.2 0.0 copy-start
  48.2 0.0 copy-start.1
  48.2 1.9 %collective-permute-start.1 = (bf16[4,288,128]{2,1,0:T(8,128)(2,1)S(1)}, bf16[4,288,128]{2,1,0:T(8,128)(2,1)S(1)}, u32[]{:S(2)}, u32[]{:S(2)}) collective-permute-start(bf16[4,288,128]{2,1,0:T(8,128)(2,1)S(1)} %get-tuple-element.17.refs_3_), channel_id=1, source_target_pairs={{0,48},{16,32},{32,16},{48,0},{64,112},{80,96},{96,80},{112,64},{1... | collective-permute-start | bytes 884744 | tf_op jit(solution)/shard_map/ppermute | solution.py:26
  50.2 1.9 %collective-permute-start = (bf16[4,288,128]{2,1,0:T(8,128)(2,1)S(1)}, bf16[4,288,128]{2,1,0:T(8,128)(2,1)S(1)}, u32[]{:S(2)}, u32[]{:S(2)}) collective-permute-start(bf16[4,288,128]{2,1,0:T(8,128)(2,1)S(1)} %get-tuple-element.18.refs_0_), channel_id=1, source_target_pairs={{0,16},{16,0},{32,48},{48,32},{64,80},{80,64},{96,112},{112,96},{1... | collective-permute-start | bytes 884744 | tf_op jit(solution)/shard_map/ppermute | solution.py:26
  52.1 5.2 %collective-permute-done.1.refs_4_ = bf16[4,288,128]{2,1,0:T(8,128)(2,1)S(1)} collective-permute-done((bf16[4,288,128]{2,1,0:T(8,128)(2,1)S(1)}, bf16[4,288,128]{2,1,0:T(8,128)(2,1)S(1)}, u32[]{:S(2)}, u32[]{:S(2)}) %collective-permute-start.1) | collective-permute-done | bytes 294944 | tf_op jit(solution)/shard_map/ppermute | solution.py:26
  57.3 0.7 collective-permute-done.refs_1_
  58.0 0.9 pad_maximum_fusion
  58.9 4.6 %collective-permute-start.2 = (bf16[2,4,288,128]{3,2,1,0:T(8,128)(2,1)}, bf16[2,4,288,128]{3,2,1,0:T(8,128)(2,1)S(1)}, u32[]{:S(2)}, u32[]{:S(2)}) collective-permute-start(bf16[2,4,288,128]{3,2,1,0:T(8,128)(2,1)} %pad_maximum_fusion), channel_id=1, source_target_pairs={{0,48},{16,32},{32,16},{48,0},{64,112},{80,96},{96,80},{112,64},{1... | collective-permute-start | bytes 1769480 | tf_op jit(solution)/shard_map/ppermute | solution.py:26
  63.5 0.9 pad_maximum_fusion.1
  64.4 1.9 %collective-permute-start.3 = (bf16[2,4,288,128]{3,2,1,0:T(8,128)(2,1)}, bf16[2,4,288,128]{3,2,1,0:T(8,128)(2,1)S(1)}, u32[]{:S(2)}, u32[]{:S(2)}) collective-permute-start(bf16[2,4,288,128]{3,2,1,0:T(8,128)(2,1)} %pad_maximum_fusion.1), channel_id=1, source_target_pairs={{0,16},{16,0},{32,48},{48,32},{64,80},{80,64},{96,112},{112,96},{1... | collective-permute-start | bytes 1769480 | tf_op jit(solution)/shard_map/ppermute | solution.py:26
  66.3 9.5 %collective-permute-start.4 = (bf16[24,128]{1,0:T(8,128)(2,1)S(1)}, bf16[24,128]{1,0:T(8,128)(2,1)S(1)}, u32[]{:S(2)}, u32[]{:S(2)}) collective-permute-start(bf16[24,128]{1,0:T(8,128)(2,1)S(1)} %reshape.14), channel_id=1, source_target_pairs={{0,1},{1,0},{2,3},{3,2},{4,5},{5,4},{6,7},{7,6},{8,9},{9,8},{10,11... | collective-permute-start | bytes 18440 | tf_op jit(solution)/shard_map/ppermute | solution.py:124
  75.8 0.8 collective-permute-done.4
  76.7 19.8 %all_to_all.17 = bf16[8,24,128]{2,1,0:T(8,128)(2,1)S(1)} all-to-all(bf16[8,24,128]{2,1,0:T(8,128)(2,1)S(1)} %broadcast_in_dim.37), channel_id=1, replica_groups={{0,2,4,6,8,10,12,14},{1,3,5,7,9,11,13,15},{16,18,20,22,24,26,28,30},{17..., dimensions={0} | all-to-all | bytes 98304 | tf_op jit(solution)/shard_map/all_to_all | solution.py:125
  96.4 0.6 reduce_sum.25
  97.0 0.0 collective-permute-done.2.refs_2_
  97.1 0.0 collective-permute-done.3.refs_5_
  97.1 0.0 all-gather.3.cloned.1.call-done
  97.1 0.0 copy-done
  97.1 0.0 copy-done.1
  97.1 0.0 copy-done.2
  97.1 0.0 copy-done.3
  97.1 0.7 copy-done.4
  97.9 0.2 copy-done.5
  98.1 5.8 %place.1 = (bf16[512,3072]{1,0:T(8,128)(2,1)}, bf16[512,3072]{1,0:T(8,128)(2,1)}) custom-call(bf16[8,4,488,128]{3,2,1,0:T(8,128)(2,1)} %bitcast.12, bf16[4,288,128]{2,1,0:T(8,128)(2,1)} %copy-done.1, bf16[4,288,128]{2,1,0:T(8,128)(2,1)} %copy-done.3, bf16[2,4,288,128]{3,2,1,0:T(8,128)(2,1)} %copy-done.4, bf16[4,288,128]{2,1,0:T(8,128)(2,1)} %copy-done, ...), custom_call_target="tpu_custom_call" | custom-call | tf_op jit(solution)/shard_map/place/pallas_call | solution.py:151
  (8 shorter events, 0.0 us)
Async XLA Ops:
  7.2 89.9 %all-gather.3.cloned.1.call-start = ((), (), s32[]{:S(2)}) async-start(), calls=%async_computation.3 | async-start | bytes 4497408 | tf_op jit(solution)/shard_map/all_gather | solution.py:117
  48.2 48.9 %copy-start = (bf16[4,288,128]{2,1,0:T(8,128)(2,1)}, bf16[4,288,128]{2,1,0:T(8,128)(2,1)S(1)}, u32[]{:S(2)}) copy-start(bf16[4,288,128]{2,1,0:T(8,128)(2,1)S(1)} %get-tuple-element.17.refs_3_) | copy-start | bytes 884740
  48.2 48.9 %copy-start.1 = (bf16[4,288,128]{2,1,0:T(8,128)(2,1)}, bf16[4,288,128]{2,1,0:T(8,128)(2,1)S(1)}, u32[]{:S(2)}) copy-start(bf16[4,288,128]{2,1,0:T(8,128)(2,1)S(1)} %get-tuple-element.18.refs_0_) | copy-start | bytes 884740
  48.2 9.1 %collective-permute-start.1 = (bf16[4,288,128]{2,1,0:T(8,128)(2,1)S(1)}, bf16[4,288,128]{2,1,0:T(8,128)(2,1)S(1)}, u32[]{:S(2)}, u32[]{:S(2)}) collective-permute-start(bf16[4,288,128]{2,1,0:T(8,128)(2,1)S(1)} %get-tuple-element.17.refs_3_), channel_id=1, source_target_pairs={{0,48},{16,32},{32,16},{48,0},{64,112},{80,96},{96,80},{112,64},{1... | collective-permute-start | bytes 884744 | tf_op jit(solution)/shard_map/ppermute | solution.py:26
  50.2 7.9 %collective-permute-start = (bf16[4,288,128]{2,1,0:T(8,128)(2,1)S(1)}, bf16[4,288,128]{2,1,0:T(8,128)(2,1)S(1)}, u32[]{:S(2)}, u32[]{:S(2)}) collective-permute-start(bf16[4,288,128]{2,1,0:T(8,128)(2,1)S(1)} %get-tuple-element.18.refs_0_), channel_id=1, source_target_pairs={{0,16},{16,0},{32,48},{48,32},{64,80},{80,64},{96,112},{112,96},{1... | collective-permute-start | bytes 884744 | tf_op jit(solution)/shard_map/ppermute | solution.py:26
  57.3 39.8 %copy-start.2 = (bf16[4,288,128]{2,1,0:T(8,128)(2,1)}, bf16[4,288,128]{2,1,0:T(8,128)(2,1)S(1)}, u32[]{:S(2)}) copy-start(bf16[4,288,128]{2,1,0:T(8,128)(2,1)S(1)} %collective-permute-done.1.refs_4_) | copy-start | bytes 884740
  58.0 39.1 %copy-start.3 = (bf16[4,288,128]{2,1,0:T(8,128)(2,1)}, bf16[4,288,128]{2,1,0:T(8,128)(2,1)S(1)}, u32[]{:S(2)}) copy-start(bf16[4,288,128]{2,1,0:T(8,128)(2,1)S(1)} %collective-permute-done.refs_1_) | copy-start | bytes 884740
  58.9 38.1 %collective-permute-start.2 = (bf16[2,4,288,128]{3,2,1,0:T(8,128)(2,1)}, bf16[2,4,288,128]{3,2,1,0:T(8,128)(2,1)S(1)}, u32[]{:S(2)}, u32[]{:S(2)}) collective-permute-start(bf16[2,4,288,128]{3,2,1,0:T(8,128)(2,1)} %pad_maximum_fusion), channel_id=1, source_target_pairs={{0,48},{16,32},{32,16},{48,0},{64,112},{80,96},{96,80},{112,64},{1... | collective-permute-start | bytes 1769480 | tf_op jit(solution)/shard_map/ppermute | solution.py:26
  64.4 32.7 %collective-permute-start.3 = (bf16[2,4,288,128]{3,2,1,0:T(8,128)(2,1)}, bf16[2,4,288,128]{3,2,1,0:T(8,128)(2,1)S(1)}, u32[]{:S(2)}, u32[]{:S(2)}) collective-permute-start(bf16[2,4,288,128]{3,2,1,0:T(8,128)(2,1)} %pad_maximum_fusion.1), channel_id=1, source_target_pairs={{0,16},{16,0},{32,48},{48,32},{64,80},{80,64},{96,112},{112,96},{1... | collective-permute-start | bytes 1769480 | tf_op jit(solution)/shard_map/ppermute | solution.py:26
  66.3 10.3 %collective-permute-start.4 = (bf16[24,128]{1,0:T(8,128)(2,1)S(1)}, bf16[24,128]{1,0:T(8,128)(2,1)S(1)}, u32[]{:S(2)}, u32[]{:S(2)}) collective-permute-start(bf16[24,128]{1,0:T(8,128)(2,1)S(1)} %reshape.14), channel_id=1, source_target_pairs={{0,1},{1,0},{2,3},{3,2},{4,5},{5,4},{6,7},{7,6},{8,9},{9,8},{10,11... | collective-permute-start | bytes 18440 | tf_op jit(solution)/shard_map/ppermute | solution.py:124
  97.0 0.8 copy-start.4
  97.1 1.0 copy-start.5
Sparse Core Ops, SparseCore 0:
  21.3 64.7 all-gather.2
